TPU v7x, 256 devices: a 8x8x2 block of a 8x8x16 slice. The times are simulated.
256 devices in a mesh: groups: 2 (over z), roll: 16 (over y, core), rows: 8 (over x).
Axes of the slice: x: 8, y: 8, z: 2, core: 2. Of those that a mesh axis runs over, the one named last changes fastest.
The devices are a block of a 8x8x16 slice.
Arguments:
- latent_slabs: bfloat16 [64, 3, 64, 8, 16], P(('groups', 'roll'), None, 'rows'), parts along dimension 0, may hold values from -18 to 18, as said below
- prior_latents: bfloat16 [64, 2, 64, 8, 16], P(('groups', 'roll'), None, 'rows'), parts along dimension 0, may hold values from -6 to 6
- prior_features: bfloat16 [64, 2, 64, 8, 512], P(('groups', 'roll'), None, 'rows'), parts along dimension 0, may hold values from -6 to 6
- lengths: int32 [64], P(('groups', 'roll')), parts along dimension 0, may hold values from 1 to 3
- starts: int32 [64], P(('groups', 'roll')), parts along dimension 0, may hold values from 0 to 6, as said below
- move_plan: int32 [64], P(('groups', 'roll')), parts along dimension 0, may hold values from -1 to 15, as said below
- entry_weight: bfloat16 [432, 512], replicated, may hold values from -0.3125 to 0.3125
- block_weight: bfloat16 [13824, 512], P(None, ('roll', 'rows')), may hold values from -0.0546875 to 0.0546875
- norm_gain: float32 [512], replicated, may hold values from 0.25 to 1.75
- norm_shift: float32 [512], replicated, may hold values from -1.2 to 1.2
Outputs:
- decoded: bfloat16 [64, 3, 64, 8, 512], P(('groups', 'roll'), None, 'rows'), parts along dimension 0
There are 2 independent parts, one for each index of `groups`. A program takes and returns all parts, laid end to end along the dimension named above; an argument that names none is the same for every part. Nothing has to cross between parts.
Inputs may be any that keep to these rules, and one draw needn't show every extreme that they name: `latent_slabs`: normal or uniform values times a scale that varies over the rows. `starts`: multiples of 3. `move_plan`: A value d * 1 + c names compute slot c of roll index d. Every compute slot of the part is named by exactly one slab, and the slabs held by one roll index name at most 1 slots of any one roll index.
All inputs are finite; a program needn't handle non-finite values.
Results may differ from a plain program's by a relative error of at most 0.0023.
Values may be sent and summed in bfloat16 or wider, within the bound.
No kernel may reach another device: no remote copies, remote signals or barrier semaphores. Data moves between devices by JAX's collectives and lax.ppermute only.
A program may use at most 128 MiB of HBM per device.

v0:
```python
import jax
import jax.numpy as jnp
from jax import lax
from jax.experimental import pallas as pl
from jax.experimental.pallas import tpu as pltpu
from jax.sharding import PartitionSpec as P

GROUPS = 32
EPSILON = 1e-06
MIB = 1 << 20


def nt_dot(a, b):
    return lax.dot_general(a, b, (((1,), (1,)), ((), ())), preferred_element_type=jnp.float32)


def latents_kernel(starts_ref, prior_hbm, new_hbm, out_ref, prior_ref, new_ref, sems):
    copies = [
        pltpu.make_async_copy(prior_hbm, prior_ref, sems.at[0]),
        pltpu.make_async_copy(new_hbm, new_ref, sems.at[1]),
    ]
    for copy in copies:
        copy.start()
    count, slots, total, height, lanes = out_ref.shape
    width, latents = prior_ref.shape[3:]
    spread = lax.broadcasted_iota(jnp.int32, (latents, lanes), 1) % latents
    spread = spread == lax.broadcasted_iota(jnp.int32, (latents, lanes), 0)
    spread = jnp.where(spread, 1.0, 0.0).astype(jnp.bfloat16)
    lane = lax.broadcasted_iota(jnp.int32, (total * height, width, lanes), 2) // latents
    col = lax.broadcasted_iota(jnp.int32, (total * height, width, lanes), 1)
    mine = lane == lax.rem(9 - col, 8)
    for copy in copies:
        copy.wait()
    for s in range(slots):
        prior = prior_ref[s]
        prior = jnp.where(starts_ref[s] > 0, prior, jnp.zeros_like(prior))
        v = jnp.concatenate([prior, new_ref[s]], axis=0).reshape(total * height * width, latents)
        v = jnp.dot(v, spread, preferred_element_type=jnp.float32)
        v = jnp.where(mine, v.reshape(total * height, width, lanes), 0.0)
        v = jnp.sum(v, axis=1).astype(jnp.bfloat16).reshape(total, height, lanes)
        for i in range(count):
            out_ref[i, s] = v


def column(n, x, roll, counts, share):
    nr, nx = counts
    piece, bit, owner = n // share, nr // 2, 0
    while bit:
        flip = piece // (nr // 2 // bit) % 2
        owner = owner + lax.rem(roll // bit + flip, 2) * bit
        bit = bit // 2
    return (owner * nx + x) * share + n % share


def hidden_kernel(counts, me_ref, roll_ref, *refs):
    outside, lat_ref, refs = refs[:3], refs[3], refs[4:]
    hid, own_ref, norm_ref, win, lhs, sums, wk_ref, wown_ref, *inside, sems = refs
    weight_ref, gain_ref, shift_ref = inside
    copies = [pltpu.make_async_copy(a, b, sems.at[i]) for i, (a, b) in enumerate(zip(outside, inside))]
    for copy in copies:
        copy.start()
    count, slots, total, height, lanes = lat_ref.shape
    frames = total - 2
    cells = count * height * 8
    features = gain_ref.shape[1]
    own = wown_ref.shape[1]
    latents = lanes // 8
    win[:, :, 0:8, :] = jnp.zeros((slots, total, 8, lanes), jnp.float32)
    win[:, :, cells + 8 : cells + 16, :] = jnp.zeros((slots, total, 8, lanes), jnp.float32)
    rows = slots * total * height
    lane = lax.broadcasted_iota(jnp.int32, (rows * 8, lanes), 1)
    col = lax.broadcasted_iota(jnp.int32, (rows * 8, lanes), 0) % 8
    first = jnp.where(col == 7, 16, 0)
    last = jnp.where(col == 0, 32, 48)
    keep = (lane >= first) & (lane < last)
    for xp in range(count):
        v = lat_ref[xp].astype(jnp.float32).reshape(rows, 1, lanes)
        v = jnp.broadcast_to(v, (rows, 8, lanes)).reshape(rows * 8, lanes)
        v = pltpu.roll(v, 0, 1, stride=16, stride_axis=0)
        v = jnp.where(keep, v, 0.0)
        v = v + pltpu.roll(v, 64, 1)
        start = 8 + xp * height * 8
        win[:, :, start : start + height * 8, :] = v.reshape(slots, total, height * 8, lanes)
    wk_ref[...] = jnp.zeros(wk_ref.shape, jnp.bfloat16)
    for copy in copies:
        copy.wait()
    for k in range(9):
        for w in range(3):
            at = k * 64 + (2 - w) * latents
            wk_ref[at : at + latents, :] = weight_ref[(k * 3 + w) * latents : (k * 3 + w + 1) * latents, :]
    place = lax.broadcasted_iota(jnp.int32, (features, own), 1)
    chosen = column(place, me_ref[0], roll_ref[0], counts, own // counts[0])
    chosen = chosen == lax.broadcasted_iota(jnp.int32, (features, own), 0)
    chosen = jnp.where(chosen, 1.0, 0.0).astype(jnp.bfloat16)
    wown_ref[...] = jnp.dot(wk_ref[...], chosen, preferred_element_type=jnp.float32).astype(jnp.bfloat16)
    low = lax.broadcasted_iota(jnp.int32, (cells, lanes), 1) < 64
    for s in range(slots):
        for f in range(frames):
            blk = s * frames + f
            for p in range(5):
                t, h = divmod(2 * p, 3)
                a = win[s, f + t, h * 8 : h * 8 + cells, :]
                if p < 4:
                    t, h = divmod(2 * p + 1, 3)
                    a = jnp.where(low, a, win[s, f + t, h * 8 : h * 8 + cells, :])
                lhs[:, p * lanes : (p + 1) * lanes] = a.astype(jnp.bfloat16)
            x = lhs[...]
            y = jnp.dot(x, wk_ref[...], preferred_element_type=jnp.float32)
            hid[s, f] = y
            sums[blk : blk + 1, :] = jnp.sum(y, axis=0, keepdims=True)
            sums[8 + blk : 9 + blk, :] = jnp.sum(y * y, axis=0, keepdims=True)
            own_ref[f, :, s * own : (s + 1) * own] = jnp.dot(
                x, wown_ref[...], preferred_element_type=jnp.float32
            )
    size = features // GROUPS
    gi = lax.broadcasted_iota(jnp.int32, (features, features), 0) // size
    gj = lax.broadcasted_iota(jnp.int32, (features, features), 1) // size
    same = jnp.where(gi == gj, 1.0, 0.0).astype(jnp.float32)
    means = jnp.dot(
        sums[...], same, precision=lax.Precision.HIGHEST, preferred_element_type=jnp.float32
    ) / (cells * size)
    mean = means[0:8]
    spread = means[8:16] - mean * mean
    scale = lax.rsqrt(spread + EPSILON) * gain_ref[...]
    norm_ref[0:8, :] = scale
    norm_ref[8:16, :] = shift_ref[...] - mean * scale


def active_kernel(hid_ref, norm_ref, act_ref):
    slots, frames = act_ref.shape[:2]

    def one(blk, carry):
        s, f = blk // frames, lax.rem(blk, frames)
        z = hid_ref[s, f] * norm_ref[pl.ds(blk, 1), :] + norm_ref[pl.ds(8 + blk, 1), :]
        act = (0.5 * z) * (1.0 + jnp.tanh(0.5 * z))
        act_ref[s, f] = act.astype(jnp.bfloat16)
        return carry

    lax.fori_loop(0, slots * frames, one, 0)


def taps_of(w_ref, t, h):
    k = w_ref.shape[1] // 27
    base = (t * 3 + h) * 3
    return jnp.concatenate([w_ref[:, (base + w) * k : (base + w + 1) * k] for w in range(3)], axis=0)


def gathered(halves, w_ref):
    for i, half in enumerate(halves):
        count, share, k = half.shape
        w_ref[i * count * share : (i + 1) * count * share, :] = half[...].reshape(count * share, k)


def new_frames(offsets, act_ref, w_ref, acc_ref):
    slots, frames, cells, _ = act_ref.shape
    for t in offsets:
        for h in range(3):
            taps = taps_of(w_ref, t, h)
            at = (2 - h) * 8
            for s in range(slots):
                for f in range(frames):
                    if 0 <= f + t - 2 < frames:
                        acc_ref[s, f, at : at + cells, :] += nt_dot(act_ref[s, f + t - 2], taps)


def first_offset_kernel(act_ref, mine_ref, other_ref, acc_ref, w_ref):
    gathered((mine_ref, other_ref), w_ref)
    acc_ref[...] = jnp.zeros(acc_ref.shape, jnp.float32)
    new_frames((2,), act_ref, w_ref, acc_ref)


def more_offsets_kernel(act_ref, w_ref, _, acc_ref):
    new_frames((1, 0), act_ref, w_ref, acc_ref)


def old_frames_kernel(count, me_ref, starts_ref, lengths_ref, plan_ref, *refs):
    feat_refs = refs[: count + 1]
    w_ref, own_ref, _ = refs[count + 1 : count + 4]
    out_refs = refs[count + 4 : 2 * count + 4]
    acc, feats, done = refs[2 * count + 4 :]
    slots, frames, padded_cells, _ = acc.shape
    own = w_ref.shape[0]
    cells = padded_cells - 16
    part = cells // count
    me = me_ref[0]
    toward = 1 - 2 * lax.rem(me, 2)
    for s in range(slots):
        for d in range(count):
            if d == count // 2:
                v = feat_refs[d if s < slots // 2 else count][s % (slots // 2)]
            else:
                v = feat_refs[d][s]
            xp = lax.rem(me + toward * d + count, count)
            start = pl.multiple_of(xp * part, part)
            feats[s, :, pl.ds(start, part), :] = jnp.where(starts_ref[s] > 0, v, jnp.zeros_like(v))
    for t in range(2):
        for h in range(3):
            at = (2 - h) * 8
            taps = taps_of(w_ref, t, h)
            for s in range(slots):
                for f in range(frames):
                    if f + t < 2:
                        acc[s, f, at : at + cells, :] += nt_dot(feats[s, f + t], taps)
    col = lax.broadcasted_iota(jnp.int32, (cells // 8, 8, own), 1)
    for f in range(frames):
        parts = []
        for s in range(slots):
            v = acc[s, f, 8 : 8 + cells, :].reshape(cells // 8, 8, 3 * own)
            left = jnp.where(col == 0, 0.0, pltpu.roll(v[:, :, 0:own], 1, 1))
            right = jnp.where(col == 7, 0.0, pltpu.roll(v[:, :, 2 * own :], 7, 1))
            v = (v[:, :, own : 2 * own] + left + right).reshape(cells, own)
            v = v + own_ref[f, :, s * own : (s + 1) * own]
            alive = (plan_ref[s] >= 0) & (f < lengths_ref[s])
            parts.append(jnp.where(alive, v, 0.0))
        done[f] = jnp.concatenate(parts, axis=1).astype(jnp.bfloat16)
    for d in range(count):
        start = pl.multiple_of(lax.rem(me + d, count) * part, part)
        out_refs[d][...] = done[:, pl.ds(start, part), :]


def columns_kernel(*refs):
    got, place_ref, out_ref = refs[:-2], refs[-2], refs[-1]
    slots, rows, features = out_ref.shape
    x = jnp.concatenate([g[...].reshape(rows, g.shape[2]) for g in got], axis=1)
    for s in range(slots):
        y = jnp.dot(
            x, place_ref[:, s * features : (s + 1) * features], preferred_element_type=jnp.float32
        )
        out_ref[s] = y.astype(jnp.bfloat16)


VMEM = pl.BlockSpec(memory_space=pltpu.VMEM)
HBM = pl.BlockSpec(memory_space=pl.ANY)
SMEM = pl.BlockSpec(memory_space=pltpu.SMEM)


def call(kernel, scalars, arrays, outs, scratch, limit, flops, aliases=None, outside=0):
    return pl.pallas_call(
        kernel,
        out_shape=outs,
        in_specs=[SMEM] * len(scalars) + [HBM] * outside + [VMEM] * (len(arrays) - outside),
        out_specs=jax.tree.map(lambda _: VMEM, outs),
        scratch_shapes=scratch,
        input_output_aliases=aliases or {},
        compiler_params=pltpu.CompilerParams(vmem_limit_bytes=limit * MIB),
        cost_estimate=pl.CostEstimate(flops=flops, bytes_accessed=1 << 22, transcendentals=0),
    )(*scalars, *arrays)


def on_device(
    latent_slabs,
    prior_latents,
    prior_features,
    lengths,
    starts,
    move_plan,
    entry_weight,
    block_weight,
    norm_gain,
    norm_shift,
):
    nx = lax.axis_size("rows")
    nr = lax.axis_size("roll")
    me = lax.axis_index("rows")
    roll = lax.axis_index("roll")
    slots, frames, height, widths, latents = latent_slabs.shape
    features = entry_weight.shape[1]
    share = block_weight.shape[1]
    own = nr * share
    part = height * widths
    cells = nx * part
    f32, bf16 = jnp.float32, jnp.bfloat16
    shape = jax.ShapeDtypeStruct
    me1 = me.reshape(1).astype(jnp.int32)
    turned = [[(i, (i + d) % nx) for i in range(nx)] for d in range(nx)]

    lat = call(
        latents_kernel,
        [starts],
        [prior_latents, latent_slabs],
        shape((nx, slots, frames + 2, height, widths * latents), bf16),
        [
            pltpu.VMEM(prior_latents.shape, bf16),
            pltpu.VMEM(latent_slabs.shape, bf16),
            pltpu.SemaphoreType.DMA((2,)),
        ],
        8,
        10_000_000,
        outside=2,
    )
    lat = lax.all_to_all(lat, "rows", 0, 0, tiled=True)

    feat = prior_features.reshape(slots, 2, part, features)
    one = [(i, i ^ 1) for i in range(nx)]
    two = [(i, (i - 1 + 2 * (i % 2)) % nx) for i in range(nx)]
    feats = [None] * (nx + 1)
    feats[0] = from_one = from_two = feat
    for k in range(1, nx // 2 + 1):
        to_one, to_two = from_two, from_one
        if 2 * k == nx:
            to_one, to_two = to_one[: slots // 2], to_two[slots // 2 :]
        feats[k] = from_one = lax.ppermute(to_one, "rows", one)
        from_two = lax.ppermute(to_two, "rows", two)
        feats[nx if 2 * k == nx else nx - k] = from_two

    wt = block_weight.T
    mine, bit = wt[None], nr // 2
    while bit > 1:
        came = lax.ppermute(mine, "roll", [(r, r ^ bit) for r in range(nr)])
        mine, bit = jnp.concatenate([mine, came], axis=0), bit // 2
    other = lax.ppermute(mine, "roll", [(r, r ^ 1) for r in range(nr)])

    line = jnp.arange(nx * slots * own)
    target = column(line % own, (me - line // (slots * own) + nx) % nx, roll, (nr, nx), share)
    target = target + line // own % slots * features
    place = (target[:, None] == jnp.arange(slots * features)[None, :]).astype(bf16)

    hid, hid_own, norm = call(
        lambda *refs: hidden_kernel((nr, nx), *refs),
        [me1, roll.reshape(1).astype(jnp.int32)],
        [entry_weight, norm_gain[None], norm_shift[None], lat],
        (
            shape((slots, frames, cells, features), f32),
            shape((frames, cells, slots * own), f32),
            shape((16, features), f32),
        ),
        [
            pltpu.VMEM((slots, frames + 2, cells + 16, widths * latents), f32),
            pltpu.VMEM((cells, 640), bf16),
            pltpu.VMEM((16, features), f32),
            pltpu.VMEM((640, features), bf16),
            pltpu.VMEM((640, own), bf16),
            pltpu.VMEM(entry_weight.shape, bf16),
            pltpu.VMEM((1, features), f32),
            pltpu.VMEM((1, features), f32),
            pltpu.SemaphoreType.DMA((3,)),
        ],
        24,
        5_000_000_000,
        outside=3,
    )
    act = call(active_kernel, [], [hid, norm], shape((slots, frames, cells, features), bf16), [], 16, 3_000_000_000)
    sums = shape((slots, frames, cells + 16, 3 * own), f32)
    acc, weights = call(
        first_offset_kernel, [], [act, mine, other], (sums, shape((own, wt.shape[1]), bf16)), [], 20, 3_000_000_000
    )
    acc = call(more_offsets_kernel, [], [act, weights, acc], sums, [], 20, 3_000_000_000, {2: 0})
    piece = shape((frames, part, slots * own), bf16)
    *pieces, _ = call(
        lambda *refs: old_frames_kernel(nx, *refs),
        [me1, starts, lengths, move_plan],
        feats + [weights, hid_own, acc],
        (piece,) * nx + (sums,),
        [
            pltpu.VMEM((slots, 2, cells, features), bf16),
            pltpu.VMEM((frames, cells, slots * own), bf16),
        ],
        30,
        3_000_000_000,
        {4 + nx + 3: nx},
    )
    got = [pieces[0]] + [lax.ppermute(pieces[d], "rows", turned[d]) for d in range(1, nx)]
    out = call(columns_kernel, [], [*got, place], shape((slots, frames * part, features), bf16), [], 20, 400_000_000)
    return out.reshape(slots, frames, height, widths, features)


def solution(mesh):
    in_specs = (
        P(("groups", "roll"), None, "rows", None, None),
        P(("groups", "roll"), None, "rows", None, None),
        P(("groups", "roll"), None, "rows", None, None),
        P(("groups", "roll")),
        P(("groups", "roll")),
        P(("groups", "roll")),
        P(),
        P(None, ("roll", "rows")),
        P(),
        P(),
    )
    out_specs = P(("groups", "roll"), None, "rows", None, None)

    return jax.shard_map(on_device, mesh=mesh, in_specs=in_specs, out_specs=out_specs, check_vma=False)
```

profile of v0, /device:TPU:518, one launch (start us, length us, event | category | flops | bytes accessed | tf_op | source)
XLA Modules:
  0.0 102.3 jit_solution(8488752403895402564)
XLA Ops:
  0.0 10.7 %collective-permute-start.8 = (bf16[1,4,13824]{2,1,0:T(4,128)(2,1)}, bf16[1,4,13824]{2,1,0:T(4,128)(2,1)S(1)}, u32[]{:S(2)}, u32[]{:S(2)}) collective-permute-start(bf16[1,4,13824]{2,1,0:T(4,128)(2,1)} %bitcast.14), channel_id=1, source_target_pairs={{0,64},{8,72},{16,80},{24,88},{32,96},{40,104},{48,112},{56,120},{... | collective-permute-start | bytes 331784 | tf_op jit(solution)/shard_map/ppermute | solution.py:309
  10.8 3.5 %collective-permute-done.8 = bf16[1,4,13824]{2,1,0:T(4,128)(2,1)S(1)} collective-permute-done((bf16[1,4,13824]{2,1,0:T(4,128)(2,1)}, bf16[1,4,13824]{2,1,0:T(4,128)(2,1)S(1)}, u32[]{:S(2)}, u32[]{:S(2)}) %collective-permute-start.8) | collective-permute-done | bytes 110624 | tf_op jit(solution)/shard_map/ppermute | solution.py:309
  14.2 1.1 %pad_maximum_fusion.2 = bf16[2,4,13824]{2,1,0:T(4,128)(2,1)S(1)} fusion(bf16[1,4,13824]{2,1,0:T(4,128)(2,1)S(1)} %collective-permute-done.8, bf16[1,4,13824]{2,1,0:T(4,128)(2,1)} %bitcast.15), kind=kLoop, calls=%fused_computation.4 | loop fusion | flops 110592 | bytes 442368 | tf_op jit(solution)/shard_map/concatenate | solution.py:310
  15.3 4.9 %collective-permute-start.9 = (bf16[2,4,13824]{2,1,0:T(4,128)(2,1)S(1)}, bf16[2,4,13824]{2,1,0:T(4,128)(2,1)S(1)}, u32[]{:S(2)}, u32[]{:S(2)}) collective-permute-start(bf16[2,4,13824]{2,1,0:T(4,128)(2,1)S(1)} %pad_maximum_fusion.2), channel_id=1, source_target_pairs={{0,32},{8,40},{16,48},{24,56},{32,0},{40,8},{48,16},{56,24},{64,96... | collective-permute-start | bytes 663560 | tf_op jit(solution)/shard_map/ppermute | solution.py:309
  20.1 9.3 %collective-permute-done.9 = bf16[2,4,13824]{2,1,0:T(4,128)(2,1)S(1)} collective-permute-done((bf16[2,4,13824]{2,1,0:T(4,128)(2,1)S(1)}, bf16[2,4,13824]{2,1,0:T(4,128)(2,1)S(1)}, u32[]{:S(2)}, u32[]{:S(2)}) %collective-permute-start.9) | collective-permute-done | bytes 221216 | tf_op jit(solution)/shard_map/ppermute | solution.py:309
  29.5 1.2 %pad_maximum_fusion.1 = bf16[4,4,13824]{2,1,0:T(4,128)(2,1)S(1)} fusion(bf16[2,4,13824]{2,1,0:T(4,128)(2,1)S(1)} %collective-permute-done.9, bf16[1,4,13824]{2,1,0:T(4,128)(2,1)S(1)} %collective-permute-done.8, bf16[1,4,13824]{2,1,0:T(4,128)(2,1)} %bitcast.16), kind=kLoop, calls=%fused_computation.3 | loop fusion | flops 442368 | bytes 884736 | tf_op jit(solution)/shard_map/concatenate | solution.py:310
  30.7 0.1 collective-permute-start.10
  30.8 3.0 %collective-permute-start.1 = (bf16[2,2,64,512]{3,2,1,0:T(8,128)(2,1)}, bf16[2,2,64,512]{3,2,1,0:T(8,128)(2,1)S(1)}, u32[]{:S(2)}, u32[]{:S(2)}) collective-permute-start(bf16[2,2,64,512]{3,2,1,0:T(8,128)(2,1)} %bitcast.9), channel_id=1, source_target_pairs={{0,7},{1,2},{2,1},{3,4},{4,3},{5,6},{6,5},{7,0},{8,15},{9,10},{10,... | collective-permute-start | bytes 786440 | tf_op jit(solution)/shard_map/ppermute | solution.py:303
  33.8 0.9 copy-done
  34.7 0.8 copy-done.1
  35.5 0.7 copy-done.2
  36.2 1.7 %shard_map.100 = bf16[8,2,5,8,128]{4,3,2,1,0:T(8,128)(2,1)} custom-call(s32[2]{0:T(128)S(1)} %copy-done.2, bf16[2,2,8,8,16]{4,3,2,1,0:T(8,128)(2,1)S(1)} %copy-done.1, bf16[2,3,8,8,16]{4,3,2,1,0:T(8,128)(2,1)S(1)} %copy-done), custom_call_target="tpu_custom_call" | custom-call | flops 10000000 | bytes 4194304 | tf_op jit(solution)/shard_map/pallas_call | solution.py:238
  37.9 9.7 %all-to-all-start = ((bf16[8,2,5,8,128]{4,3,2,1,0:T(8,128)(2,1)}), bf16[8,2,5,8,128]{4,3,2,1,0:T(8,128)(2,1)S(1)}, u32[]{:S(2)}, u32[]{:S(2)}) async-start(bf16[8,2,5,8,128]{4,3,2,1,0:T(8,128)(2,1)} %shard_map.100), calls=%async_computation | async-start | bytes 327680 | tf_op jit(solution)/shard_map/all_to_all | solution.py:291
  47.6 0.0 collective-permute-done.10
  47.6 1.5 %pad_maximum_fusion.mine_ref = bf16[8,4,13824]{2,1,0:T(4,128)(2,1)S(1)} fusion(bf16[4,4,13824]{2,1,0:T(4,128)(2,1)S(1)} %collective-permute-done.10, bf16[2,4,13824]{2,1,0:T(4,128)(2,1)S(1)} %collective-permute-done.9, bf16[1,4,13824]{2,1,0:T(4,128)(2,1)S(1)} %collective-permute-done.8, bf16[1,4,13824]{2,1,0:T(4,128)(2,1)} %bitcast.17), kind=kLoop, calls=%fused_computation.2 | loop fusion | flops 1327104 | bytes 1769472 | tf_op jit(solution)/shard_map/concatenate | solution.py:310
  49.2 0.1 collective-permute-start.11
  49.4 0.7 collective-permute-start.2
  50.0 0.0 collective-permute-done.refs_5_
  50.0 2.7 %collective-permute-start.3 = (bf16[2,2,64,512]{3,2,1,0:T(8,128)(2,1)S(1)}, bf16[2,2,64,512]{3,2,1,0:T(8,128)(2,1)S(1)}, u32[]{:S(2)}, u32[]{:S(2)}) collective-permute-start(bf16[2,2,64,512]{3,2,1,0:T(8,128)(2,1)S(1)} %collective-permute-done.refs_5_), channel_id=1, source_target_pairs={{0,7},{1,2},{2,1},{3,4},{4,3},{5,6},{6,5},{7,0},{8,15},{9,10},{10,... | collective-permute-start | bytes 786440 | tf_op jit(solution)/shard_map/ppermute | solution.py:303
  52.7 0.8 all-to-all-done.refs_5_
  53.6 6.5 %shard_map.101 = (f32[2,3,512,512]{3,2,1,0:T(8,128)S(1)}, f32[3,512,128]{2,1,0:T(8,128)S(1)}, f32[16,512]{1,0:T(8,128)S(1)}) custom-call(s32[1]{0:T(128)} %bitcast.refs_0_, s32[1]{0:T(128)} %bitcast.2.refs_1_, bf16[432,512]{1,0:T(8,128)(2,1)S(1)} %copy-done.4, f32[1,512]{1,0:T(1,128)S(1)} %bitcast.12, f32[1,512]{1,0:T(1,128)S(1)} %bitcast.13, ...), custom_call_target="tpu_custom_call" | custom-call | flops 5000000000 | bytes 4194304 | tf_op jit(solution)/shard_map/pallas_call | solution.py:238
  60.1 0.0 collective-permute-done.2.refs_6_
  60.1 0.9 collective-permute-start.5
  61.0 0.0 collective-permute-done.3.refs_10_
  61.0 2.4 %collective-permute-start.4 = (bf16[2,2,64,512]{3,2,1,0:T(8,128)(2,1)S(1)}, bf16[2,2,64,512]{3,2,1,0:T(8,128)(2,1)S(1)}, u32[]{:S(2)}, u32[]{:S(2)}) collective-permute-start(bf16[2,2,64,512]{3,2,1,0:T(8,128)(2,1)S(1)} %collective-permute-done.3.refs_10_), channel_id=1, source_target_pairs={{0,1},{1,0},{2,3},{3,2},{4,5},{5,4},{6,7},{7,6},{8,9},{9,8},{10,11... | collective-permute-start | bytes 786440 | tf_op jit(solution)/shard_map/ppermute | solution.py:302
  63.4 1.4 %shard_map.102.act_ref = bf16[2,3,512,512]{3,2,1,0:T(8,128)(2,1)S(1)} custom-call(f32[2,3,512,512]{3,2,1,0:T(8,128)S(1)} %get-tuple-element.18.hid_ref, f32[16,512]{1,0:T(8,128)S(1)} %get-tuple-element.19.norm_ref), custom_call_target="tpu_custom_call" | custom-call | flops 3000000000 | bytes 4194304 | tf_op jit(solution)/shard_map/pallas_call | solution.py:238
  64.9 3.8 %collective-permute-done.5.refs_9_ = bf16[2,2,64,512]{3,2,1,0:T(8,128)(2,1)S(1)} collective-permute-done((bf16[2,2,64,512]{3,2,1,0:T(8,128)(2,1)S(1)}, bf16[2,2,64,512]{3,2,1,0:T(8,128)(2,1)S(1)}, u32[]{:S(2)}, u32[]{:S(2)}) %collective-permute-start.5) | collective-permute-done | bytes 262176 | tf_op jit(solution)/shard_map/ppermute | solution.py:303
  68.6 0.1 collective-permute-start.6
  68.8 0.0 collective-permute-done.4.refs_7_
  68.8 1.9 %collective-permute-start.7 = (bf16[1,2,64,512]{3,2,1,0:T(8,128)(2,1)S(1)}, bf16[1,2,64,512]{3,2,1,0:T(8,128)(2,1)S(1)}, u32[]{:S(2)}, u32[]{:S(2)}) collective-permute-start(bf16[1,2,64,512]{3,2,1,0:T(8,128)(2,1)S(1)} %slice.9), channel_id=1, source_target_pairs={{0,7},{1,2},{2,1},{3,4},{4,3},{5,6},{6,5},{7,0},{8,15},{9,10},{10,... | collective-permute-start | bytes 393224 | tf_op jit(solution)/shard_map/ppermute | solution.py:303
  70.7 2.8 %shard_map.103 = (f32[2,3,528,192]{3,2,1,0:T(8,128)S(1)}, bf16[64,13824]{1,0:T(8,128)(2,1)S(1)}) custom-call(bf16[2,3,512,512]{3,2,1,0:T(8,128)(2,1)S(1)} %shard_map.102.act_ref, bf16[8,4,13824]{2,1,0:T(4,128)(2,1)S(1)} %pad_maximum_fusion.mine_ref, bf16[8,4,13824]{2,1,0:T(4,128)(2,1)S(1)} %collective-permute-done.11.other_ref), custom_call_target="tpu_custom_call" | custom-call | flops 3000000000 | bytes 4194304 | tf_op jit(solution)/shard_map/pallas_call | solution.py:238
  73.5 0.0 copy-start.3
  73.5 0.0 copy-start.5
  73.6 0.0 copy-start.8
  73.6 0.0 copy-start.9
  73.6 2.6 %shard_map.104.refs_15_ = f32[2,3,528,192]{3,2,1,0:T(8,128)S(1)} custom-call(bf16[2,3,512,512]{3,2,1,0:T(8,128)(2,1)S(1)} %shard_map.102.act_ref, bf16[64,13824]{1,0:T(8,128)(2,1)S(1)} %get-tuple-element.20.w_ref.refs_13_, f32[2,3,528,192]{3,2,1,0:T(8,128)S(1)} %get-tuple-element.22._), custom_call_target="tpu_custom_call", output_to_operand_aliasing={{}: (2, {})} | custom-call | flops 3000000000 | bytes 4194304 | tf_op jit(solution)/shard_map/pallas_call | solution.py:238
  76.3 3.8 %shard_map.105 = (bf16[3,64,128]{2,1,0:T(8,128)(2,1)S(1)}, bf16[3,64,128]{2,1,0:T(8,128)(2,1)S(1)}, bf16[3,64,128]{2,1,0:T(8,128)(2,1)S(1)}, bf16[3,64,128]{2,1,...) custom-call(s32[1]{0:T(128)} %bitcast.refs_0_, ...), custom_call_target="tpu_custom_call", output_to_operand_aliasing={{8}: (15, {})} | custom-call | flops 3000000000 | bytes 4194304 | tf_op jit(solution)/shard_map/pallas_call | solution.py:238
  80.1 1.8 %collective-permute-start.12 = (bf16[3,64,128]{2,1,0:T(8,128)(2,1)S(1)}, bf16[3,64,128]{2,1,0:T(8,128)(2,1)S(1)}, u32[]{:S(2)}, u32[]{:S(2)}) collective-permute-start(bf16[3,64,128]{2,1,0:T(8,128)(2,1)S(1)} %get-tuple-element.24), channel_id=1, source_target_pairs={{0,1},{1,2},{2,3},{3,4},{4,5},{5,6},{6,7},{7,0},{8,9},{9,10},{10,1... | collective-permute-start | bytes 147464 | tf_op jit(solution)/shard_map/ppermute | solution.py:362
  81.9 1.2 %collective-permute-start.13 = (bf16[3,64,128]{2,1,0:T(8,128)(2,1)S(1)}, bf16[3,64,128]{2,1,0:T(8,128)(2,1)S(1)}, u32[]{:S(2)}, u32[]{:S(2)}) collective-permute-start(bf16[3,64,128]{2,1,0:T(8,128)(2,1)S(1)} %get-tuple-element.25), channel_id=1, source_target_pairs={{0,2},{1,3},{2,4},{3,5},{4,6},{5,7},{6,0},{7,1},{8,10},{9,11},{10,... | collective-permute-start | bytes 147464 | tf_op jit(solution)/shard_map/ppermute | solution.py:362
  83.2 4.6 %collective-permute-start.14 = (bf16[3,64,128]{2,1,0:T(8,128)(2,1)S(1)}, bf16[3,64,128]{2,1,0:T(8,128)(2,1)S(1)}, u32[]{:S(2)}, u32[]{:S(2)}) collective-permute-start(bf16[3,64,128]{2,1,0:T(8,128)(2,1)S(1)} %get-tuple-element.26), channel_id=1, source_target_pairs={{0,3},{1,4},{2,5},{3,6},{4,7},{5,0},{6,1},{7,2},{8,11},{9,12},{10,... | collective-permute-start | bytes 147464 | tf_op jit(solution)/shard_map/ppermute | solution.py:362
  87.8 1.8 %collective-permute-start.15 = (bf16[3,64,128]{2,1,0:T(8,128)(2,1)S(1)}, bf16[3,64,128]{2,1,0:T(8,128)(2,1)S(1)}, u32[]{:S(2)}, u32[]{:S(2)}) collective-permute-start(bf16[3,64,128]{2,1,0:T(8,128)(2,1)S(1)} %get-tuple-element.27), channel_id=1, source_target_pairs={{0,4},{1,5},{2,6},{3,7},{4,0},{5,1},{6,2},{7,3},{8,12},{9,13},{10,... | collective-permute-start | bytes 147464 | tf_op jit(solution)/shard_map/ppermute | solution.py:362
  89.6 2.2 %collective-permute-start.16 = (bf16[3,64,128]{2,1,0:T(8,128)(2,1)S(1)}, bf16[3,64,128]{2,1,0:T(8,128)(2,1)S(1)}, u32[]{:S(2)}, u32[]{:S(2)}) collective-permute-start(bf16[3,64,128]{2,1,0:T(8,128)(2,1)S(1)} %get-tuple-element.28), channel_id=1, source_target_pairs={{0,5},{1,6},{2,7},{3,0},{4,1},{5,2},{6,3},{7,4},{8,13},{9,14},{10,... | collective-permute-start | bytes 147464 | tf_op jit(solution)/shard_map/ppermute | solution.py:362
  91.8 3.8 %collective-permute-start.17 = (bf16[3,64,128]{2,1,0:T(8,128)(2,1)S(1)}, bf16[3,64,128]{2,1,0:T(8,128)(2,1)S(1)}, u32[]{:S(2)}, u32[]{:S(2)}) collective-permute-start(bf16[3,64,128]{2,1,0:T(8,128)(2,1)S(1)} %get-tuple-element.29), channel_id=1, source_target_pairs={{0,6},{1,7},{2,0},{3,1},{4,2},{5,3},{6,4},{7,5},{8,14},{9,15},{10,... | collective-permute-start | bytes 147464 | tf_op jit(solution)/shard_map/ppermute | solution.py:362
  95.6 0.4 fusion.refs_8_
  96.1 1.3 %collective-permute-done.16.refs_5_ = bf16[3,64,128]{2,1,0:T(8,128)(2,1)S(1)} collective-permute-done((bf16[3,64,128]{2,1,0:T(8,128)(2,1)S(1)}, bf16[3,64,128]{2,1,0:T(8,128)(2,1)S(1)}, u32[]{:S(2)}, u32[]{:S(2)}) %collective-permute-start.16) | collective-permute-done | bytes 49184 | tf_op jit(solution)/shard_map/ppermute | solution.py:362
  97.4 0.7 collective-permute-done.17.refs_6_
  98.1 2.8 %collective-permute-done.18.refs_7_ = bf16[3,64,128]{2,1,0:T(8,128)(2,1)S(1)} collective-permute-done((bf16[3,64,128]{2,1,0:T(8,128)(2,1)S(1)}, bf16[3,64,128]{2,1,0:T(8,128)(2,1)S(1)}, u32[]{:S(2)}, u32[]{:S(2)}) %collective-permute-start.18) | collective-permute-done | bytes 49184 | tf_op jit(solution)/shard_map/ppermute | solution.py:362
  100.9 1.3 %shard_map.106 = bf16[2,192,512]{2,1,0:T(8,128)(2,1)} custom-call(bf16[3,64,128]{2,1,0:T(8,128)(2,1)S(1)} %get-tuple-element.23.refs_0_, bf16[3,64,128]{2,1,0:T(8,128)(2,1)S(1)} %collective-permute-done.12.refs_1_, bf16[3,64,128]{2,1,0:T(8,128)(2,1)S(1)} %collective-permute-done.13.refs_2_, bf16[3,64,128]{2,1,0:T(8,128)(2,1)S(1)} %collective-permute-done.14.refs_3_, ...), custom_call_target="tpu_custom_call" | custom-call | flops 400000000 | bytes 4194304 | tf_op jit(solution)/shard_map/pallas_call | solution.py:238
  (26 shorter events, 0.1 us)
Async XLA Ops:
  0.0 53.6 %copy-start.6 = (f32[512]{0:T(512)S(1)}, f32[512]{0:T(512)}, u32[]{:S(2)}) copy-start(f32[512]{0:T(512)} %param.18) | copy-start | bytes 6148
  0.0 53.6 %copy-start.7 = (f32[512]{0:T(512)S(1)}, f32[512]{0:T(512)}, u32[]{:S(2)}) copy-start(f32[512]{0:T(512)} %param.19) | copy-start | bytes 6148
  0.0 53.6 %copy-start.4 = (bf16[432,512]{1,0:T(8,128)(2,1)S(1)}, bf16[432,512]{1,0:T(8,128)(2,1)}, u32[]{:S(2)}) copy-start(bf16[432,512]{1,0:T(8,128)(2,1)} %refs_2_.2) | copy-start | bytes 1327108
  0.0 14.2 %collective-permute-start.8 = (bf16[1,4,13824]{2,1,0:T(4,128)(2,1)}, bf16[1,4,13824]{2,1,0:T(4,128)(2,1)S(1)}, u32[]{:S(2)}, u32[]{:S(2)}) collective-permute-start(bf16[1,4,13824]{2,1,0:T(4,128)(2,1)} %bitcast.14), channel_id=1, source_target_pairs={{0,64},{8,72},{16,80},{24,88},{32,96},{40,104},{48,112},{56,120},{... | collective-permute-start | bytes 331784 | tf_op jit(solution)/shard_map/ppermute | solution.py:309
  15.3 14.2 %collective-permute-start.9 = (bf16[2,4,13824]{2,1,0:T(4,128)(2,1)S(1)}, bf16[2,4,13824]{2,1,0:T(4,128)(2,1)S(1)}, u32[]{:S(2)}, u32[]{:S(2)}) collective-permute-start(bf16[2,4,13824]{2,1,0:T(4,128)(2,1)S(1)} %pad_maximum_fusion.2), channel_id=1, source_target_pairs={{0,32},{8,40},{16,48},{24,56},{32,0},{40,8},{48,16},{56,24},{64,96... | collective-permute-start | bytes 663560 | tf_op jit(solution)/shard_map/ppermute | solution.py:309
  30.7 16.9 %collective-permute-start.10 = (bf16[4,4,13824]{2,1,0:T(4,128)(2,1)S(1)}, bf16[4,4,13824]{2,1,0:T(4,128)(2,1)S(1)}, u32[]{:S(2)}, u32[]{:S(2)}) collective-permute-start(bf16[4,4,13824]{2,1,0:T(4,128)(2,1)S(1)} %pad_maximum_fusion.1), channel_id=1, source_target_pairs={{0,16},{8,24},{16,0},{24,8},{32,48},{40,56},{48,32},{56,40},{64,80... | collective-permute-start | bytes 1327112 | tf_op jit(solution)/shard_map/ppermute | solution.py:309
  30.8 18.5 %collective-permute-start.1 = (bf16[2,2,64,512]{3,2,1,0:T(8,128)(2,1)}, bf16[2,2,64,512]{3,2,1,0:T(8,128)(2,1)S(1)}, u32[]{:S(2)}, u32[]{:S(2)}) collective-permute-start(bf16[2,2,64,512]{3,2,1,0:T(8,128)(2,1)} %bitcast.9), channel_id=1, source_target_pairs={{0,7},{1,2},{2,1},{3,4},{4,3},{5,6},{6,5},{7,0},{8,15},{9,10},{10,... | collective-permute-start | bytes 786440 | tf_op jit(solution)/shard_map/ppermute | solution.py:303
  33.8 16.2 %collective-permute-start = (bf16[2,2,64,512]{3,2,1,0:T(8,128)(2,1)}, bf16[2,2,64,512]{3,2,1,0:T(8,128)(2,1)S(1)}, u32[]{:S(2)}, u32[]{:S(2)}) collective-permute-start(bf16[2,2,64,512]{3,2,1,0:T(8,128)(2,1)} %bitcast.10), channel_id=1, source_target_pairs={{0,1},{1,0},{2,3},{3,2},{4,5},{5,4},{6,7},{7,6},{8,9},{9,8},{10,11... | collective-permute-start | bytes 786440 | tf_op jit(solution)/shard_map/ppermute | solution.py:302
  33.8 0.9 copy-start
  34.7 0.8 copy-start.1
  35.5 0.7 copy-start.2
  37.9 15.7 %all-to-all-start = ((bf16[8,2,5,8,128]{4,3,2,1,0:T(8,128)(2,1)}), bf16[8,2,5,8,128]{4,3,2,1,0:T(8,128)(2,1)S(1)}, u32[]{:S(2)}, u32[]{:S(2)}) async-start(bf16[8,2,5,8,128]{4,3,2,1,0:T(8,128)(2,1)} %shard_map.100), calls=%async_computation | async-start | bytes 327680 | tf_op jit(solution)/shard_map/all_to_all | solution.py:291
  49.2 21.6 %collective-permute-start.11 = (bf16[8,4,13824]{2,1,0:T(4,128)(2,1)S(1)}, bf16[8,4,13824]{2,1,0:T(4,128)(2,1)S(1)}, u32[]{:S(2)}, u32[]{:S(2)}) collective-permute-start(bf16[8,4,13824]{2,1,0:T(4,128)(2,1)S(1)} %pad_maximum_fusion.mine_ref), channel_id=1, source_target_pairs={{0,8},{8,0},{16,24},{24,16},{32,40},{40,32},{48,56},{56,48},{64,72... | collective-permute-start | bytes 2654216 | tf_op jit(solution)/shard_map/ppermute | solution.py:311
  49.4 10.8 %collective-permute-start.2 = (bf16[2,2,64,512]{3,2,1,0:T(8,128)(2,1)S(1)}, bf16[2,2,64,512]{3,2,1,0:T(8,128)(2,1)S(1)}, u32[]{:S(2)}, u32[]{:S(2)}) collective-permute-start(bf16[2,2,64,512]{3,2,1,0:T(8,128)(2,1)S(1)} %collective-permute-done.1.refs_11_), channel_id=1, source_target_pairs={{0,1},{1,0},{2,3},{3,2},{4,5},{5,4},{6,7},{7,6},{8,9},{9,8},{10,11... | collective-permute-start | bytes 786440 | tf_op jit(solution)/shard_map/ppermute | solution.py:302
  50.0 11.0 %collective-permute-start.3 = (bf16[2,2,64,512]{3,2,1,0:T(8,128)(2,1)S(1)}, bf16[2,2,64,512]{3,2,1,0:T(8,128)(2,1)S(1)}, u32[]{:S(2)}, u32[]{:S(2)}) collective-permute-start(bf16[2,2,64,512]{3,2,1,0:T(8,128)(2,1)S(1)} %collective-permute-done.refs_5_), channel_id=1, source_target_pairs={{0,7},{1,2},{2,1},{3,4},{4,3},{5,6},{6,5},{7,0},{8,15},{9,10},{10,... | collective-permute-start | bytes 786440 | tf_op jit(solution)/shard_map/ppermute | solution.py:303
  60.1 8.5 %collective-permute-start.5 = (bf16[2,2,64,512]{3,2,1,0:T(8,128)(2,1)S(1)}, bf16[2,2,64,512]{3,2,1,0:T(8,128)(2,1)S(1)}, u32[]{:S(2)}, u32[]{:S(2)}) collective-permute-start(bf16[2,2,64,512]{3,2,1,0:T(8,128)(2,1)S(1)} %collective-permute-done.2.refs_6_), channel_id=1, source_target_pairs={{0,7},{1,2},{2,1},{3,4},{4,3},{5,6},{6,5},{7,0},{8,15},{9,10},{10,... | collective-permute-start | bytes 786440 | tf_op jit(solution)/shard_map/ppermute | solution.py:303
  61.0 7.7 %collective-permute-start.4 = (bf16[2,2,64,512]{3,2,1,0:T(8,128)(2,1)S(1)}, bf16[2,2,64,512]{3,2,1,0:T(8,128)(2,1)S(1)}, u32[]{:S(2)}, u32[]{:S(2)}) collective-permute-start(bf16[2,2,64,512]{3,2,1,0:T(8,128)(2,1)S(1)} %collective-permute-done.3.refs_10_), channel_id=1, source_target_pairs={{0,1},{1,0},{2,3},{3,2},{4,5},{5,4},{6,7},{7,6},{8,9},{9,8},{10,11... | collective-permute-start | bytes 786440 | tf_op jit(solution)/shard_map/ppermute | solution.py:302
  68.6 7.6 %collective-permute-start.6 = (bf16[1,2,64,512]{3,2,1,0:T(8,128)(2,1)S(1)}, bf16[1,2,64,512]{3,2,1,0:T(8,128)(2,1)S(1)}, u32[]{:S(2)}, u32[]{:S(2)}) collective-permute-start(bf16[1,2,64,512]{3,2,1,0:T(8,128)(2,1)S(1)} %slice.8), channel_id=1, source_target_pairs={{0,1},{1,0},{2,3},{3,2},{4,5},{5,4},{6,7},{7,6},{8,9},{9,8},{10,11... | collective-permute-start | bytes 393224 | tf_op jit(solution)/shard_map/ppermute | solution.py:302
  68.8 7.4 %collective-permute-start.7 = (bf16[1,2,64,512]{3,2,1,0:T(8,128)(2,1)S(1)}, bf16[1,2,64,512]{3,2,1,0:T(8,128)(2,1)S(1)}, u32[]{:S(2)}, u32[]{:S(2)}) collective-permute-start(bf16[1,2,64,512]{3,2,1,0:T(8,128)(2,1)S(1)} %slice.9), channel_id=1, source_target_pairs={{0,7},{1,2},{2,1},{3,4},{4,3},{5,6},{6,5},{7,0},{8,15},{9,10},{10,... | collective-permute-start | bytes 393224 | tf_op jit(solution)/shard_map/ppermute | solution.py:303
  73.5 2.7 %copy-start.3 = (s32[2]{0:T(128)S(1)}, s32[2]{0:T(128)}, u32[]{:S(2)}) copy-start(s32[2]{0:T(128)} %refs_1_.1) | copy-start | bytes 28
  73.5 2.7 %copy-start.5 = (bf16[2,2,8,8,512]{4,3,2,1,0:T(8,128)(2,1)S(1)}, bf16[2,2,8,8,512]{4,3,2,1,0:T(8,128)(2,1)}, u32[]{:S(2)}) copy-start(bf16[2,2,8,8,512]{4,3,2,1,0:T(8,128)(2,1)} %param.12) | copy-start | bytes 786436
  73.6 2.7 %copy-start.8 = (s32[2]{0:T(128)S(1)}, s32[2]{0:T(128)}, u32[]{:S(2)}) copy-start(s32[2]{0:T(128)} %refs_2_.3) | copy-start | bytes 28
  73.6 2.7 %copy-start.9 = (s32[2]{0:T(128)S(1)}, s32[2]{0:T(128)}, u32[]{:S(2)}) copy-start(s32[2]{0:T(128)} %refs_3_.1) | copy-start | bytes 28
  80.1 11.7 %collective-permute-start.12 = (bf16[3,64,128]{2,1,0:T(8,128)(2,1)S(1)}, bf16[3,64,128]{2,1,0:T(8,128)(2,1)S(1)}, u32[]{:S(2)}, u32[]{:S(2)}) collective-permute-start(bf16[3,64,128]{2,1,0:T(8,128)(2,1)S(1)} %get-tuple-element.24), channel_id=1, source_target_pairs={{0,1},{1,2},{2,3},{3,4},{4,5},{5,6},{6,7},{7,0},{8,9},{9,10},{10,1... | collective-permute-start | bytes 147464 | tf_op jit(solution)/shard_map/ppermute | solution.py:362
  81.9 13.7 %collective-permute-start.13 = (bf16[3,64,128]{2,1,0:T(8,128)(2,1)S(1)}, bf16[3,64,128]{2,1,0:T(8,128)(2,1)S(1)}, u32[]{:S(2)}, u32[]{:S(2)}) collective-permute-start(bf16[3,64,128]{2,1,0:T(8,128)(2,1)S(1)} %get-tuple-element.25), channel_id=1, source_target_pairs={{0,2},{1,3},{2,4},{3,5},{4,6},{5,7},{6,0},{7,1},{8,10},{9,11},{10,... | collective-permute-start | bytes 147464 | tf_op jit(solution)/shard_map/ppermute | solution.py:362
  83.2 12.9 %collective-permute-start.14 = (bf16[3,64,128]{2,1,0:T(8,128)(2,1)S(1)}, bf16[3,64,128]{2,1,0:T(8,128)(2,1)S(1)}, u32[]{:S(2)}, u32[]{:S(2)}) collective-permute-start(bf16[3,64,128]{2,1,0:T(8,128)(2,1)S(1)} %get-tuple-element.26), channel_id=1, source_target_pairs={{0,3},{1,4},{2,5},{3,6},{4,7},{5,0},{6,1},{7,2},{8,11},{9,12},{10,... | collective-permute-start | bytes 147464 | tf_op jit(solution)/shard_map/ppermute | solution.py:362
  87.8 8.3 %collective-permute-start.15 = (bf16[3,64,128]{2,1,0:T(8,128)(2,1)S(1)}, bf16[3,64,128]{2,1,0:T(8,128)(2,1)S(1)}, u32[]{:S(2)}, u32[]{:S(2)}) collective-permute-start(bf16[3,64,128]{2,1,0:T(8,128)(2,1)S(1)} %get-tuple-element.27), channel_id=1, source_target_pairs={{0,4},{1,5},{2,6},{3,7},{4,0},{5,1},{6,2},{7,3},{8,12},{9,13},{10,... | collective-permute-start | bytes 147464 | tf_op jit(solution)/shard_map/ppermute | solution.py:362
  89.6 7.7 %collective-permute-start.16 = (bf16[3,64,128]{2,1,0:T(8,128)(2,1)S(1)}, bf16[3,64,128]{2,1,0:T(8,128)(2,1)S(1)}, u32[]{:S(2)}, u32[]{:S(2)}) collective-permute-start(bf16[3,64,128]{2,1,0:T(8,128)(2,1)S(1)} %get-tuple-element.28), channel_id=1, source_target_pairs={{0,5},{1,6},{2,7},{3,0},{4,1},{5,2},{6,3},{7,4},{8,13},{9,14},{10,... | collective-permute-start | bytes 147464 | tf_op jit(solution)/shard_map/ppermute | solution.py:362
  91.8 6.3 %collective-permute-start.17 = (bf16[3,64,128]{2,1,0:T(8,128)(2,1)S(1)}, bf16[3,64,128]{2,1,0:T(8,128)(2,1)S(1)}, u32[]{:S(2)}, u32[]{:S(2)}) collective-permute-start(bf16[3,64,128]{2,1,0:T(8,128)(2,1)S(1)} %get-tuple-element.29), channel_id=1, source_target_pairs={{0,6},{1,7},{2,0},{3,1},{4,2},{5,3},{6,4},{7,5},{8,14},{9,15},{10,... | collective-permute-start | bytes 147464 | tf_op jit(solution)/shard_map/ppermute | solution.py:362
  95.6 5.3 %collective-permute-start.18 = (bf16[3,64,128]{2,1,0:T(8,128)(2,1)S(1)}, bf16[3,64,128]{2,1,0:T(8,128)(2,1)S(1)}, u32[]{:S(2)}, u32[]{:S(2)}) collective-permute-start(bf16[3,64,128]{2,1,0:T(8,128)(2,1)S(1)} %get-tuple-element.30), channel_id=1, source_target_pairs={{0,7},{1,0},{2,1},{3,2},{4,3},{5,4},{6,5},{7,6},{8,15},{9,8},{10,9... | collective-permute-start | bytes 147464 | tf_op jit(solution)/shard_map/ppermute | solution.py:362
where the time goes:
time: 103 us; the launch traced here: 102 us
  starting transfers between devices  52.8 us (51%)
  waiting for transfers between devices  22.3 us (22%)
  Pallas kernels  20.3 us (20%)
  other arithmetic  4.24 us (4%)
  local copies, waits for them, and re-layouts  2.44 us (2%)
    pallas_call x7, Pallas kernels, call(): pl.pallas_call(kernel, out_shape=outs, in_specs=[SMEM] * len(scalars) + [...  20.3 us
    ppermute x3, starting transfers between devices, on_device(): came = lax.ppermute(mine, 'roll', [(r, r ^ bit) for r in range(nr)])  15.7 us
    ppermute x7, starting transfers between devices, on_device(): lax.ppermute(pieces[d], 'rows', turned[d])  15.5 us
    ppermute x3, waiting for transfers between devices, on_device(): came = lax.ppermute(mine, 'roll', [(r, r ^ bit) for r in range(nr)])  12.8 us
    all_to_all x1, starting transfers between devices, on_device(): lat = lax.all_to_all(lat, 'rows', 0, 0, tiled=True)  9.74 us
    ppermute x4, starting transfers between devices, on_device(): from_two = lax.ppermute(to_two, 'rows', two)  8.48 us
    ppermute x7, waiting for transfers between devices, on_device(): lax.ppermute(pieces[d], 'rows', turned[d])  4.87 us
    concatenate x3, other arithmetic, on_device(): mine, bit = (jnp.concatenate([mine, came], axis=0), bit // 2)  3.8 us
  transfers between devices with their start and end apart: 20, of which 7 were waited for; matrix products, arithmetic and copies ran while one was open for 2% of the time, Pallas kernels for 15%

commit v1 on v0

--- a/solution.py
+++ b/solution.py
@@ -14,14 +14,14 @@
     return lax.dot_general(a, b, (((1,), (1,)), ((), ())), preferred_element_type=jnp.float32)
 
 
-def latents_kernel(starts_ref, prior_hbm, new_hbm, out_ref, prior_ref, new_ref, sems):
+def latents_kernel(prior_hbm, new_hbm, out_ref, prior_ref, new_ref, sems):
     copies = [
         pltpu.make_async_copy(prior_hbm, prior_ref, sems.at[0]),
         pltpu.make_async_copy(new_hbm, new_ref, sems.at[1]),
     ]
     for copy in copies:
         copy.start()
-    count, slots, total, height, lanes = out_ref.shape
+    _, slots, total, height, lanes = out_ref.shape
     width, latents = prior_ref.shape[3:]
     spread = lax.broadcasted_iota(jnp.int32, (latents, lanes), 1) % latents
     spread = spread == lax.broadcasted_iota(jnp.int32, (latents, lanes), 0)
@@ -32,34 +32,28 @@
     for copy in copies:
         copy.wait()
     for s in range(slots):
-        prior = prior_ref[s]
-        prior = jnp.where(starts_ref[s] > 0, prior, jnp.zeros_like(prior))
-        v = jnp.concatenate([prior, new_ref[s]], axis=0).reshape(total * height * width, latents)
+        v = jnp.concatenate([prior_ref[s], new_ref[s]], axis=0).reshape(total * height * width, latents)
         v = jnp.dot(v, spread, preferred_element_type=jnp.float32)
         v = jnp.where(mine, v.reshape(total * height, width, lanes), 0.0)
-        v = jnp.sum(v, axis=1).astype(jnp.bfloat16).reshape(total, height, lanes)
-        for i in range(count):
-            out_ref[i, s] = v
+        out_ref[0, s] = jnp.sum(v, axis=1).astype(jnp.bfloat16).reshape(total, height, lanes)
 
 
 def column(n, x, roll, counts, share):
     nr, nx = counts
-    piece, bit, owner = n // share, nr // 2, 0
-    while bit:
-        flip = piece // (nr // 2 // bit) % 2
-        owner = owner + lax.rem(roll // bit + flip, 2) * bit
-        bit = bit // 2
+    piece = n // share
+    owner = piece % (nr // 2) * 2 + lax.rem(roll + piece // (nr // 2), 2)
     return (owner * nx + x) * share + n % share
 
 
-def hidden_kernel(counts, me_ref, roll_ref, *refs):
-    outside, lat_ref, refs = refs[:3], refs[3], refs[4:]
+def hidden_kernel(counts, me_ref, roll_ref, starts_ref, *refs):
+    outside, lat_refs, refs = refs[:3], refs[3:5], refs[5:]
     hid, own_ref, norm_ref, win, lhs, sums, wk_ref, wown_ref, *inside, sems = refs
     weight_ref, gain_ref, shift_ref = inside
     copies = [pltpu.make_async_copy(a, b, sems.at[i]) for i, (a, b) in enumerate(zip(outside, inside))]
     for copy in copies:
         copy.start()
-    count, slots, total, height, lanes = lat_ref.shape
+    count = counts[1]
+    slots, total, height, lanes = lat_refs[0].shape[1:]
     frames = total - 2
     cells = count * height * 8
     features = gain_ref.shape[1]
@@ -67,20 +61,26 @@
     latents = lanes // 8
     win[:, :, 0:8, :] = jnp.zeros((slots, total, 8, lanes), jnp.float32)
     win[:, :, cells + 8 : cells + 16, :] = jnp.zeros((slots, total, 8, lanes), jnp.float32)
-    rows = slots * total * height
+    rows = total * height
     lane = lax.broadcasted_iota(jnp.int32, (rows * 8, lanes), 1)
     col = lax.broadcasted_iota(jnp.int32, (rows * 8, lanes), 0) % 8
     first = jnp.where(col == 7, 16, 0)
     last = jnp.where(col == 0, 32, 48)
     keep = (lane >= first) & (lane < last)
-    for xp in range(count):
-        v = lat_ref[xp].astype(jnp.float32).reshape(rows, 1, lanes)
-        v = jnp.broadcast_to(v, (rows, 8, lanes)).reshape(rows * 8, lanes)
-        v = pltpu.roll(v, 0, 1, stride=16, stride_axis=0)
-        v = jnp.where(keep, v, 0.0)
-        v = v + pltpu.roll(v, 64, 1)
-        start = 8 + xp * height * 8
-        win[:, :, start : start + height * 8, :] = v.reshape(slots, total, height * 8, lanes)
+    frame = lax.broadcasted_iota(jnp.int32, (total, height, lanes), 0)
+    for p in range(count):
+        bit, flip = 1, 0
+        while bit < count:
+            flip, bit = flip + (p * 2 * bit // count % 2) * bit, bit * 2
+        start = pl.multiple_of(8 + (me_ref[0] ^ flip) * (height * 8), 8)
+        for s in range(slots):
+            v = lat_refs[p * 2 // count][p % (count // 2), s].astype(jnp.float32)
+            v = jnp.where((frame > 1) | (starts_ref[s] > 0), v, 0.0).reshape(rows, 1, lanes)
+            v = jnp.broadcast_to(v, (rows, 8, lanes)).reshape(rows * 8, lanes)
+            v = pltpu.roll(v, 0, 1, stride=16, stride_axis=0)
+            v = jnp.where(keep, v, 0.0)
+            v = v + pltpu.roll(v, 64, 1)
+            win[s, :, pl.ds(start, height * 8), :] = v.reshape(total, height * 8, lanes)
     wk_ref[...] = jnp.zeros(wk_ref.shape, jnp.bfloat16)
     for copy in copies:
         copy.wait()
@@ -230,7 +230,7 @@
 
 
 VMEM = pl.BlockSpec(memory_space=pltpu.VMEM)
-HBM = pl.BlockSpec(memory_space=pl.ANY)
+HBM = pl.BlockSpec(memory_space=pltpu.HBM)
 SMEM = pl.BlockSpec(memory_space=pltpu.SMEM)
 
 
@@ -276,9 +276,9 @@
 
     lat = call(
         latents_kernel,
-        [starts],
+        [],
         [prior_latents, latent_slabs],
-        shape((nx, slots, frames + 2, height, widths * latents), bf16),
+        shape((1, slots, frames + 2, height, widths * latents), bf16),
         [
             pltpu.VMEM(prior_latents.shape, bf16),
             pltpu.VMEM(latent_slabs.shape, bf16),
@@ -288,7 +288,13 @@
         10_000_000,
         outside=2,
     )
-    lat = lax.all_to_all(lat, "rows", 0, 0, tiled=True)
+    bit = nx // 2
+    while bit:
+        came = lax.ppermute(lat, "rows", [(i, i ^ bit) for i in range(nx)])
+        if bit > 1:
+            lat = jnp.concatenate([lat, came], axis=0)
+        bit = bit // 2
+    lats = [lat, came]
 
     feat = prior_features.reshape(slots, 2, part, features)
     one = [(i, i ^ 1) for i in range(nx)]
@@ -304,10 +310,9 @@
         feats[nx if 2 * k == nx else nx - k] = from_two
 
     wt = block_weight.T
-    mine, bit = wt[None], nr // 2
-    while bit > 1:
-        came = lax.ppermute(mine, "roll", [(r, r ^ bit) for r in range(nr)])
-        mine, bit = jnp.concatenate([mine, came], axis=0), bit // 2
+    same_core = [[r for r in range(nr) if r % 2 == c] for c in range(2)]
+    mine = jnp.broadcast_to(wt[None], (nr // 2, *wt.shape))
+    mine = lax.all_to_all(mine, "roll", 0, 0, axis_index_groups=same_core, tiled=True)
     other = lax.ppermute(mine, "roll", [(r, r ^ 1) for r in range(nr)])
 
     line = jnp.arange(nx * slots * own)
@@ -317,8 +322,8 @@
 
     hid, hid_own, norm = call(
         lambda *refs: hidden_kernel((nr, nx), *refs),
-        [me1, roll.reshape(1).astype(jnp.int32)],
-        [entry_weight, norm_gain[None], norm_shift[None], lat],
+        [me1, roll.reshape(1).astype(jnp.int32), starts],
+        [entry_weight, norm_gain[None], norm_shift[None], *lats],
         (
             shape((slots, frames, cells, features), f32),
             shape((frames, cells, slots * own), f32),

time: 103 us -> 98.7 us (0.958)
  the two profiles are of different devices: /device:TPU:518 before, /device:TPU:640 now
where the time goes in v1:
time: 98.7 us; the launch traced here: 98.3 us
  starting transfers between devices  50.4 us (51%)
  waiting for transfers between devices  20.6 us (21%)
  Pallas kernels  19.8 us (20%)
  local copies, waits for them, and re-layouts  6.85 us (7%)
    pallas_call x7, Pallas kernels, call(): pl.pallas_call(kernel, out_shape=outs, in_specs=[SMEM] * len(scalars) + [...  19.8 us
    ppermute x7, starting transfers between devices, on_device(): lax.ppermute(pieces[d], 'rows', turned[d])  15.4 us
    all_to_all x1, starting transfers between devices, on_device(): lax.all_to_all(mine, 'roll', 0, 0, axis_index_groups=same_core, tiled=True)  13.2 us
    all_to_all x1, waiting for transfers between devices, on_device(): lax.all_to_all(mine, 'roll', 0, 0, axis_index_groups=same_core, tiled=True)  12.5 us
    ppermute x3, starting transfers between devices, on_device(): came = lax.ppermute(lat, 'rows', [(i, i ^ bit) for i in range(nx)])  10.6 us
    ppermute x4, starting transfers between devices, on_device(): from_two = lax.ppermute(to_two, 'rows', two)  9.64 us
    unnamed x20, local copies, waits for them, and re-layouts  4.78 us
    ppermute x4, waiting for transfers between devices, on_device(): from_two = lax.ppermute(to_two, 'rows', two)  4.36 us
  transfers between devices with their start and end apart: 20, of which 7 were waited for; matrix products, arithmetic and copies ran while one was open for 0% of the time, Pallas kernels for 15%

profile of v1, /device:TPU:640, one launch (start us, length us, event | category | flops | bytes accessed | tf_op | source)
XLA Modules:
  0.0 98.3 jit_solution(12792110279444255045)
XLA Ops:
  0.0 2.0 %broadcast_in_dim.16 = bf16[8,4,13824]{2,1,0:T(4,128)(2,1)} broadcast(bf16[4,13824]{1,0:T(4,128)(2,1)} %bitcast.12), dimensions={1,2} | broadcast | bytes 995328 | tf_op jit(solution)/shard_map/broadcast_in_dim | solution.py:314
  2.0 13.2 %all-to-all-start = ((bf16[8,4,13824]{2,1,0:T(4,128)(2,1)}), bf16[8,4,13824]{2,1,0:T(4,128)(2,1)S(1)}, u32[]{:S(2)}, u32[]{:S(2)}) async-start(bf16[8,4,13824]{2,1,0:T(4,128)(2,1)} %broadcast_in_dim.16), calls=%async_computation | async-start | bytes 1769472 | tf_op jit(solution)/shard_map/all_to_all | solution.py:315
  15.2 0.9 copy-done
  16.1 0.8 copy-done.1
  16.9 0.4 shard_map.100
  17.4 6.2 %collective-permute-start.8 = (bf16[1,2,5,8,128]{4,3,2,1,0:T(8,128)(2,1)S(1)}, bf16[1,2,5,8,128]{4,3,2,1,0:T(8,128)(2,1)S(1)}, u32[]{:S(2)}, u32[]{:S(2)}) collective-permute-start(bf16[1,2,5,8,128]{4,3,2,1,0:T(8,128)(2,1)S(1)} %shard_map.100), channel_id=1, source_target_pairs={{0,4},{1,5},{2,6},{3,7},{4,0},{5,1},{6,2},{7,3},{8,12},{9,13},{10,... | collective-permute-start | bytes 61448 | tf_op jit(solution)/shard_map/ppermute | solution.py:293
  23.5 0.4 collective-permute-start.1
  23.9 1.0 %collective-permute-start = (bf16[2,2,64,512]{3,2,1,0:T(8,128)(2,1)}, bf16[2,2,64,512]{3,2,1,0:T(8,128)(2,1)S(1)}, u32[]{:S(2)}, u32[]{:S(2)}) collective-permute-start(bf16[2,2,64,512]{3,2,1,0:T(8,128)(2,1)} %bitcast.8), channel_id=1, source_target_pairs={{0,1},{1,0},{2,3},{3,2},{4,5},{5,4},{6,7},{7,6},{8,9},{9,8},{10,11... | collective-permute-start | bytes 786440 | tf_op jit(solution)/shard_map/ppermute | solution.py:308
  25.0 0.3 collective-permute-done.8
  25.3 2.7 %collective-permute-start.9 = (bf16[2,2,5,8,128]{4,3,2,1,0:T(8,128)(2,1)S(1)}, bf16[2,2,5,8,128]{4,3,2,1,0:T(8,128)(2,1)S(1)}, u32[]{:S(2)}, u32[]{:S(2)}) collective-permute-start(bf16[2,2,5,8,128]{4,3,2,1,0:T(8,128)(2,1)S(1)} %pad_maximum_fusion.1), channel_id=1, source_target_pairs={{0,2},{1,3},{2,0},{3,1},{4,6},{5,7},{6,4},{7,5},{8,10},{9,11},{10,... | collective-permute-start | bytes 122888 | tf_op jit(solution)/shard_map/ppermute | solution.py:293
  28.0 12.5 %all-to-all-done.mine_ref = bf16[8,4,13824]{2,1,0:T(4,128)(2,1)S(1)} async-done(((bf16[8,4,13824]{2,1,0:T(4,128)(2,1)}), bf16[8,4,13824]{2,1,0:T(4,128)(2,1)S(1)}, u32[]{:S(2)}, u32[]{:S(2)}) %all-to-all-start) | async-done | bytes 884768 | tf_op jit(solution)/shard_map/all_to_all | solution.py:315
  40.5 0.0 collective-permute-start.11
  40.5 1.8 %collective-permute-start.10 = (bf16[4,2,5,8,128]{4,3,2,1,0:T(8,128)(2,1)S(1)}, bf16[4,2,5,8,128]{4,3,2,1,0:T(8,128)(2,1)S(1)}, u32[]{:S(2)}, u32[]{:S(2)}) collective-permute-start(bf16[4,2,5,8,128]{4,3,2,1,0:T(8,128)(2,1)S(1)} %pad_maximum_fusion.refs_6_), channel_id=1, source_target_pairs={{0,1},{1,0},{2,3},{3,2},{4,5},{5,4},{6,7},{7,6},{8,9},{9,8},{10,11... | collective-permute-start | bytes 245768 | tf_op jit(solution)/shard_map/ppermute | solution.py:293
  42.3 0.4 collective-permute-start.2
  42.7 3.8 %collective-permute-start.3 = (bf16[2,2,64,512]{3,2,1,0:T(8,128)(2,1)S(1)}, bf16[2,2,64,512]{3,2,1,0:T(8,128)(2,1)S(1)}, u32[]{:S(2)}, u32[]{:S(2)}) collective-permute-start(bf16[2,2,64,512]{3,2,1,0:T(8,128)(2,1)S(1)} %collective-permute-done.refs_5_), channel_id=1, source_target_pairs={{0,7},{1,2},{2,1},{3,4},{4,3},{5,6},{6,5},{7,0},{8,15},{9,10},{10,... | collective-permute-start | bytes 786440 | tf_op jit(solution)/shard_map/ppermute | solution.py:309
  46.5 1.0 %copy-done.2 = bf16[432,512]{1,0:T(8,128)(2,1)S(1)} copy-done((bf16[432,512]{1,0:T(8,128)(2,1)S(1)}, bf16[432,512]{1,0:T(8,128)(2,1)}, u32[]{:S(2)}) %copy-start.2) | copy-done | bytes 442392
  47.5 0.7 copy-done.4
  48.2 0.7 copy-done.5
  48.9 0.7 copy-done.6
  49.5 7.4 %shard_map.101 = (f32[2,3,512,512]{3,2,1,0:T(8,128)S(1)}, f32[3,512,128]{2,1,0:T(8,128)S(1)}, f32[16,512]{1,0:T(8,128)S(1)}) custom-call(s32[1]{0:T(128)} %bitcast.refs_0_, s32[1]{0:T(128)} %bitcast.2.refs_1_, s32[2]{0:T(128)S(1)} %copy-done.6, bf16[432,512]{1,0:T(8,128)(2,1)S(1)} %copy-done.2, f32[1,512]{1,0:T(1,128)S(1)} %bitcast.10, ...), custom_call_target="tpu_custom_call" | custom-call | flops 5000000000 | bytes 4194304 | tf_op jit(solution)/shard_map/pallas_call | solution.py:238
  56.9 3.6 %collective-permute-start.5 = (bf16[2,2,64,512]{3,2,1,0:T(8,128)(2,1)S(1)}, bf16[2,2,64,512]{3,2,1,0:T(8,128)(2,1)S(1)}, u32[]{:S(2)}, u32[]{:S(2)}) collective-permute-start(bf16[2,2,64,512]{3,2,1,0:T(8,128)(2,1)S(1)} %collective-permute-done.2.refs_6_), channel_id=1, source_target_pairs={{0,7},{1,2},{2,1},{3,4},{4,3},{5,6},{6,5},{7,0},{8,15},{9,10},{10,... | collective-permute-start | bytes 786440 | tf_op jit(solution)/shard_map/ppermute | solution.py:309
  60.5 0.0 collective-permute-start.4
  60.5 1.4 %shard_map.102.act_ref = bf16[2,3,512,512]{3,2,1,0:T(8,128)(2,1)S(1)} custom-call(f32[2,3,512,512]{3,2,1,0:T(8,128)S(1)} %get-tuple-element.18.hid_ref, f32[16,512]{1,0:T(8,128)S(1)} %get-tuple-element.19.norm_ref), custom_call_target="tpu_custom_call" | custom-call | flops 3000000000 | bytes 4194304 | tf_op jit(solution)/shard_map/pallas_call | solution.py:238
  61.9 4.4 %collective-permute-done.5.refs_9_ = bf16[2,2,64,512]{3,2,1,0:T(8,128)(2,1)S(1)} collective-permute-done((bf16[2,2,64,512]{3,2,1,0:T(8,128)(2,1)S(1)}, bf16[2,2,64,512]{3,2,1,0:T(8,128)(2,1)S(1)}, u32[]{:S(2)}, u32[]{:S(2)}) %collective-permute-start.5) | collective-permute-done | bytes 262176 | tf_op jit(solution)/shard_map/ppermute | solution.py:309
  66.3 0.1 collective-permute-start.6
  66.5 1.1 %collective-permute-done.4.refs_7_ = bf16[2,2,64,512]{3,2,1,0:T(8,128)(2,1)S(1)} collective-permute-done((bf16[2,2,64,512]{3,2,1,0:T(8,128)(2,1)S(1)}, bf16[2,2,64,512]{3,2,1,0:T(8,128)(2,1)S(1)}, u32[]{:S(2)}, u32[]{:S(2)}) %collective-permute-start.4) | collective-permute-done | bytes 262176 | tf_op jit(solution)/shard_map/ppermute | solution.py:308
  67.6 1.8 %collective-permute-start.7 = (bf16[1,2,64,512]{3,2,1,0:T(8,128)(2,1)S(1)}, bf16[1,2,64,512]{3,2,1,0:T(8,128)(2,1)S(1)}, u32[]{:S(2)}, u32[]{:S(2)}) collective-permute-start(bf16[1,2,64,512]{3,2,1,0:T(8,128)(2,1)S(1)} %slice.9), channel_id=1, source_target_pairs={{0,7},{1,2},{2,1},{3,4},{4,3},{5,6},{6,5},{7,0},{8,15},{9,10},{10,... | collective-permute-start | bytes 393224 | tf_op jit(solution)/shard_map/ppermute | solution.py:309
  69.4 2.8 %shard_map.103 = (f32[2,3,528,192]{3,2,1,0:T(8,128)S(1)}, bf16[64,13824]{1,0:T(8,128)(2,1)S(1)}) custom-call(bf16[2,3,512,512]{3,2,1,0:T(8,128)(2,1)S(1)} %shard_map.102.act_ref, bf16[8,4,13824]{2,1,0:T(4,128)(2,1)S(1)} %all-to-all-done.mine_ref, bf16[8,4,13824]{2,1,0:T(4,128)(2,1)S(1)} %collective-permute-done.11.other_ref), custom_call_target="tpu_custom_call" | custom-call | flops 3000000000 | bytes 4194304 | tf_op jit(solution)/shard_map/pallas_call | solution.py:238
  72.3 0.0 copy-start.3
  72.3 0.0 copy-start.7
  72.3 0.0 copy-start.8
  72.3 0.0 copy-start.9
  72.3 2.6 %shard_map.104.refs_15_ = f32[2,3,528,192]{3,2,1,0:T(8,128)S(1)} custom-call(bf16[2,3,512,512]{3,2,1,0:T(8,128)(2,1)S(1)} %shard_map.102.act_ref, bf16[64,13824]{1,0:T(8,128)(2,1)S(1)} %get-tuple-element.20.w_ref.refs_13_, f32[2,3,528,192]{3,2,1,0:T(8,128)S(1)} %get-tuple-element.22._), custom_call_target="tpu_custom_call", output_to_operand_aliasing={{}: (2, {})} | custom-call | flops 3000000000 | bytes 4194304 | tf_op jit(solution)/shard_map/pallas_call | solution.py:238
  75.0 3.8 %shard_map.105 = (bf16[3,64,128]{2,1,0:T(8,128)(2,1)S(1)}, bf16[3,64,128]{2,1,0:T(8,128)(2,1)S(1)}, bf16[3,64,128]{2,1,0:T(8,128)(2,1)S(1)}, bf16[3,64,128]{2,1,...) custom-call(s32[1]{0:T(128)} %bitcast.refs_0_, ...), custom_call_target="tpu_custom_call", output_to_operand_aliasing={{8}: (15, {})} | custom-call | flops 3000000000 | bytes 4194304 | tf_op jit(solution)/shard_map/pallas_call | solution.py:238
  78.9 1.1 %collective-permute-start.12 = (bf16[3,64,128]{2,1,0:T(8,128)(2,1)S(1)}, bf16[3,64,128]{2,1,0:T(8,128)(2,1)S(1)}, u32[]{:S(2)}, u32[]{:S(2)}) collective-permute-start(bf16[3,64,128]{2,1,0:T(8,128)(2,1)S(1)} %get-tuple-element.24), channel_id=1, source_target_pairs={{0,1},{1,2},{2,3},{3,4},{4,5},{5,6},{6,7},{7,0},{8,9},{9,10},{10,1... | collective-permute-start | bytes 147464 | tf_op jit(solution)/shard_map/ppermute | solution.py:367
  80.0 2.3 %collective-permute-start.13 = (bf16[3,64,128]{2,1,0:T(8,128)(2,1)S(1)}, bf16[3,64,128]{2,1,0:T(8,128)(2,1)S(1)}, u32[]{:S(2)}, u32[]{:S(2)}) collective-permute-start(bf16[3,64,128]{2,1,0:T(8,128)(2,1)S(1)} %get-tuple-element.25), channel_id=1, source_target_pairs={{0,2},{1,3},{2,4},{3,5},{4,6},{5,7},{6,0},{7,1},{8,10},{9,11},{10,... | collective-permute-start | bytes 147464 | tf_op jit(solution)/shard_map/ppermute | solution.py:367
  82.3 3.0 %collective-permute-start.14 = (bf16[3,64,128]{2,1,0:T(8,128)(2,1)S(1)}, bf16[3,64,128]{2,1,0:T(8,128)(2,1)S(1)}, u32[]{:S(2)}, u32[]{:S(2)}) collective-permute-start(bf16[3,64,128]{2,1,0:T(8,128)(2,1)S(1)} %get-tuple-element.26), channel_id=1, source_target_pairs={{0,3},{1,4},{2,5},{3,6},{4,7},{5,0},{6,1},{7,2},{8,11},{9,12},{10,... | collective-permute-start | bytes 147464 | tf_op jit(solution)/shard_map/ppermute | solution.py:367
  85.3 0.9 collective-permute-start.15
  86.2 3.7 %collective-permute-start.16 = (bf16[3,64,128]{2,1,0:T(8,128)(2,1)S(1)}, bf16[3,64,128]{2,1,0:T(8,128)(2,1)S(1)}, u32[]{:S(2)}, u32[]{:S(2)}) collective-permute-start(bf16[3,64,128]{2,1,0:T(8,128)(2,1)S(1)} %get-tuple-element.28), channel_id=1, source_target_pairs={{0,5},{1,6},{2,7},{3,0},{4,1},{5,2},{6,3},{7,4},{8,13},{9,14},{10,... | collective-permute-start | bytes 147464 | tf_op jit(solution)/shard_map/ppermute | solution.py:367
  89.9 0.0 collective-permute-done.12.refs_1_
  89.9 2.7 %collective-permute-start.17 = (bf16[3,64,128]{2,1,0:T(8,128)(2,1)S(1)}, bf16[3,64,128]{2,1,0:T(8,128)(2,1)S(1)}, u32[]{:S(2)}, u32[]{:S(2)}) collective-permute-start(bf16[3,64,128]{2,1,0:T(8,128)(2,1)S(1)} %get-tuple-element.29), channel_id=1, source_target_pairs={{0,6},{1,7},{2,0},{3,1},{4,2},{5,3},{6,4},{7,5},{8,14},{9,15},{10,... | collective-permute-start | bytes 147464 | tf_op jit(solution)/shard_map/ppermute | solution.py:367
  92.6 0.0 collective-permute-done.13.refs_2_
  92.6 1.7 %collective-permute-start.18 = (bf16[3,64,128]{2,1,0:T(8,128)(2,1)S(1)}, bf16[3,64,128]{2,1,0:T(8,128)(2,1)S(1)}, u32[]{:S(2)}, u32[]{:S(2)}) collective-permute-start(bf16[3,64,128]{2,1,0:T(8,128)(2,1)S(1)} %get-tuple-element.30), channel_id=1, source_target_pairs={{0,7},{1,0},{2,1},{3,2},{4,3},{5,4},{6,5},{7,6},{8,15},{9,8},{10,9... | collective-permute-start | bytes 147464 | tf_op jit(solution)/shard_map/ppermute | solution.py:367
  94.3 0.4 fusion.refs_8_
  94.7 0.2 collective-permute-done.16.refs_5_
  94.9 1.6 %collective-permute-done.17.refs_6_ = bf16[3,64,128]{2,1,0:T(8,128)(2,1)S(1)} collective-permute-done((bf16[3,64,128]{2,1,0:T(8,128)(2,1)S(1)}, bf16[3,64,128]{2,1,0:T(8,128)(2,1)S(1)}, u32[]{:S(2)}, u32[]{:S(2)}) %collective-permute-start.17) | collective-permute-done | bytes 49184 | tf_op jit(solution)/shard_map/ppermute | solution.py:367
  96.5 0.5 collective-permute-done.18.refs_7_
  97.0 1.3 %shard_map.106 = bf16[2,192,512]{2,1,0:T(8,128)(2,1)} custom-call(bf16[3,64,128]{2,1,0:T(8,128)(2,1)S(1)} %get-tuple-element.23.refs_0_, bf16[3,64,128]{2,1,0:T(8,128)(2,1)S(1)} %collective-permute-done.12.refs_1_, bf16[3,64,128]{2,1,0:T(8,128)(2,1)S(1)} %collective-permute-done.13.refs_2_, bf16[3,64,128]{2,1,0:T(8,128)(2,1)S(1)} %collective-permute-done.14.refs_3_, ...), custom_call_target="tpu_custom_call" | custom-call | flops 400000000 | bytes 4194304 | tf_op jit(solution)/shard_map/pallas_call | solution.py:238
  (26 shorter events, 0.1 us)
Async XLA Ops:
  2.0 38.4 %all-to-all-start = ((bf16[8,4,13824]{2,1,0:T(4,128)(2,1)}), bf16[8,4,13824]{2,1,0:T(4,128)(2,1)S(1)}, u32[]{:S(2)}, u32[]{:S(2)}) async-start(bf16[8,4,13824]{2,1,0:T(4,128)(2,1)} %broadcast_in_dim.16), calls=%async_computation | async-start | bytes 1769472 | tf_op jit(solution)/shard_map/all_to_all | solution.py:315
  15.2 0.9 copy-start
  16.1 0.8 copy-start.1
  17.4 7.9 %collective-permute-start.8 = (bf16[1,2,5,8,128]{4,3,2,1,0:T(8,128)(2,1)S(1)}, bf16[1,2,5,8,128]{4,3,2,1,0:T(8,128)(2,1)S(1)}, u32[]{:S(2)}, u32[]{:S(2)}) collective-permute-start(bf16[1,2,5,8,128]{4,3,2,1,0:T(8,128)(2,1)S(1)} %shard_map.100), channel_id=1, source_target_pairs={{0,4},{1,5},{2,6},{3,7},{4,0},{5,1},{6,2},{7,3},{8,12},{9,13},{10,... | collective-permute-start | bytes 61448 | tf_op jit(solution)/shard_map/ppermute | solution.py:293
  23.5 18.7 %collective-permute-start.1 = (bf16[2,2,64,512]{3,2,1,0:T(8,128)(2,1)}, bf16[2,2,64,512]{3,2,1,0:T(8,128)(2,1)S(1)}, u32[]{:S(2)}, u32[]{:S(2)}) collective-permute-start(bf16[2,2,64,512]{3,2,1,0:T(8,128)(2,1)} %bitcast.7), channel_id=1, source_target_pairs={{0,7},{1,2},{2,1},{3,4},{4,3},{5,6},{6,5},{7,0},{8,15},{9,10},{10,... | collective-permute-start | bytes 786440 | tf_op jit(solution)/shard_map/ppermute | solution.py:309
  23.9 18.7 %collective-permute-start = (bf16[2,2,64,512]{3,2,1,0:T(8,128)(2,1)}, bf16[2,2,64,512]{3,2,1,0:T(8,128)(2,1)S(1)}, u32[]{:S(2)}, u32[]{:S(2)}) collective-permute-start(bf16[2,2,64,512]{3,2,1,0:T(8,128)(2,1)} %bitcast.8), channel_id=1, source_target_pairs={{0,1},{1,0},{2,3},{3,2},{4,5},{5,4},{6,7},{7,6},{8,9},{9,8},{10,11... | collective-permute-start | bytes 786440 | tf_op jit(solution)/shard_map/ppermute | solution.py:308
  25.3 15.2 %collective-permute-start.9 = (bf16[2,2,5,8,128]{4,3,2,1,0:T(8,128)(2,1)S(1)}, bf16[2,2,5,8,128]{4,3,2,1,0:T(8,128)(2,1)S(1)}, u32[]{:S(2)}, u32[]{:S(2)}) collective-permute-start(bf16[2,2,5,8,128]{4,3,2,1,0:T(8,128)(2,1)S(1)} %pad_maximum_fusion.1), channel_id=1, source_target_pairs={{0,2},{1,3},{2,0},{3,1},{4,6},{5,7},{6,4},{7,5},{8,10},{9,11},{10,... | collective-permute-start | bytes 122888 | tf_op jit(solution)/shard_map/ppermute | solution.py:293
  40.5 29.0 %collective-permute-start.11 = (bf16[8,4,13824]{2,1,0:T(4,128)(2,1)S(1)}, bf16[8,4,13824]{2,1,0:T(4,128)(2,1)S(1)}, u32[]{:S(2)}, u32[]{:S(2)}) collective-permute-start(bf16[8,4,13824]{2,1,0:T(4,128)(2,1)S(1)} %all-to-all-done.mine_ref), channel_id=1, source_target_pairs={{0,8},{8,0},{16,24},{24,16},{32,40},{40,32},{48,56},{56,48},{64,72... | collective-permute-start | bytes 2654216 | tf_op jit(solution)/shard_map/ppermute | solution.py:316
  40.5 6.0 %collective-permute-start.10 = (bf16[4,2,5,8,128]{4,3,2,1,0:T(8,128)(2,1)S(1)}, bf16[4,2,5,8,128]{4,3,2,1,0:T(8,128)(2,1)S(1)}, u32[]{:S(2)}, u32[]{:S(2)}) collective-permute-start(bf16[4,2,5,8,128]{4,3,2,1,0:T(8,128)(2,1)S(1)} %pad_maximum_fusion.refs_6_), channel_id=1, source_target_pairs={{0,1},{1,0},{2,3},{3,2},{4,5},{5,4},{6,7},{7,6},{8,9},{9,8},{10,11... | collective-permute-start | bytes 245768 | tf_op jit(solution)/shard_map/ppermute | solution.py:293
  42.3 14.6 %collective-permute-start.2 = (bf16[2,2,64,512]{3,2,1,0:T(8,128)(2,1)S(1)}, bf16[2,2,64,512]{3,2,1,0:T(8,128)(2,1)S(1)}, u32[]{:S(2)}, u32[]{:S(2)}) collective-permute-start(bf16[2,2,64,512]{3,2,1,0:T(8,128)(2,1)S(1)} %collective-permute-done.1.refs_11_), channel_id=1, source_target_pairs={{0,1},{1,0},{2,3},{3,2},{4,5},{5,4},{6,7},{7,6},{8,9},{9,8},{10,11... | collective-permute-start | bytes 786440 | tf_op jit(solution)/shard_map/ppermute | solution.py:308
  42.7 17.8 %collective-permute-start.3 = (bf16[2,2,64,512]{3,2,1,0:T(8,128)(2,1)S(1)}, bf16[2,2,64,512]{3,2,1,0:T(8,128)(2,1)S(1)}, u32[]{:S(2)}, u32[]{:S(2)}) collective-permute-start(bf16[2,2,64,512]{3,2,1,0:T(8,128)(2,1)S(1)} %collective-permute-done.refs_5_), channel_id=1, source_target_pairs={{0,7},{1,2},{2,1},{3,4},{4,3},{5,6},{6,5},{7,0},{8,15},{9,10},{10,... | collective-permute-start | bytes 786440 | tf_op jit(solution)/shard_map/ppermute | solution.py:309
  46.5 1.0 %copy-start.2 = (bf16[432,512]{1,0:T(8,128)(2,1)S(1)}, bf16[432,512]{1,0:T(8,128)(2,1)}, u32[]{:S(2)}) copy-start(bf16[432,512]{1,0:T(8,128)(2,1)} %refs_3_.2) | copy-start | bytes 1327108
  47.5 0.7 copy-start.4
  48.2 0.7 copy-start.5
  48.9 0.7 copy-start.6
  56.9 9.4 %collective-permute-start.5 = (bf16[2,2,64,512]{3,2,1,0:T(8,128)(2,1)S(1)}, bf16[2,2,64,512]{3,2,1,0:T(8,128)(2,1)S(1)}, u32[]{:S(2)}, u32[]{:S(2)}) collective-permute-start(bf16[2,2,64,512]{3,2,1,0:T(8,128)(2,1)S(1)} %collective-permute-done.2.refs_6_), channel_id=1, source_target_pairs={{0,7},{1,2},{2,1},{3,4},{4,3},{5,6},{6,5},{7,0},{8,15},{9,10},{10,... | collective-permute-start | bytes 786440 | tf_op jit(solution)/shard_map/ppermute | solution.py:309
  60.5 7.1 %collective-permute-start.4 = (bf16[2,2,64,512]{3,2,1,0:T(8,128)(2,1)S(1)}, bf16[2,2,64,512]{3,2,1,0:T(8,128)(2,1)S(1)}, u32[]{:S(2)}, u32[]{:S(2)}) collective-permute-start(bf16[2,2,64,512]{3,2,1,0:T(8,128)(2,1)S(1)} %collective-permute-done.3.refs_10_), channel_id=1, source_target_pairs={{0,1},{1,0},{2,3},{3,2},{4,5},{5,4},{6,7},{7,6},{8,9},{9,8},{10,11... | collective-permute-start | bytes 786440 | tf_op jit(solution)/shard_map/ppermute | solution.py:308
  66.3 8.7 %collective-permute-start.6 = (bf16[1,2,64,512]{3,2,1,0:T(8,128)(2,1)S(1)}, bf16[1,2,64,512]{3,2,1,0:T(8,128)(2,1)S(1)}, u32[]{:S(2)}, u32[]{:S(2)}) collective-permute-start(bf16[1,2,64,512]{3,2,1,0:T(8,128)(2,1)S(1)} %slice.8), channel_id=1, source_target_pairs={{0,1},{1,0},{2,3},{3,2},{4,5},{5,4},{6,7},{7,6},{8,9},{9,8},{10,11... | collective-permute-start | bytes 393224 | tf_op jit(solution)/shard_map/ppermute | solution.py:308
  67.6 7.4 %collective-permute-start.7 = (bf16[1,2,64,512]{3,2,1,0:T(8,128)(2,1)S(1)}, bf16[1,2,64,512]{3,2,1,0:T(8,128)(2,1)S(1)}, u32[]{:S(2)}, u32[]{:S(2)}) collective-permute-start(bf16[1,2,64,512]{3,2,1,0:T(8,128)(2,1)S(1)} %slice.9), channel_id=1, source_target_pairs={{0,7},{1,2},{2,1},{3,4},{4,3},{5,6},{6,5},{7,0},{8,15},{9,10},{10,... | collective-permute-start | bytes 393224 | tf_op jit(solution)/shard_map/ppermute | solution.py:309
  72.3 2.7 %copy-start.3 = (bf16[2,2,8,8,512]{4,3,2,1,0:T(8,128)(2,1)S(1)}, bf16[2,2,8,8,512]{4,3,2,1,0:T(8,128)(2,1)}, u32[]{:S(2)}) copy-start(bf16[2,2,8,8,512]{4,3,2,1,0:T(8,128)(2,1)} %param.12) | copy-start | bytes 786436
  72.3 2.7 %copy-start.7 = (s32[2]{0:T(128)S(1)}, s32[2]{0:T(128)}, u32[]{:S(2)}) copy-start(s32[2]{0:T(128)} %refs_1_.1) | copy-start | bytes 28
  72.3 2.7 %copy-start.8 = (s32[2]{0:T(128)S(1)}, s32[2]{0:T(128)}, u32[]{:S(2)}) copy-start(s32[2]{0:T(128)} %refs_2_.3) | copy-start | bytes 28
  72.3 2.7 %copy-start.9 = (s32[2]{0:T(128)S(1)}, s32[2]{0:T(128)}, u32[]{:S(2)}) copy-start(s32[2]{0:T(128)} %refs_3_.3) | copy-start | bytes 28
  78.9 11.0 %collective-permute-start.12 = (bf16[3,64,128]{2,1,0:T(8,128)(2,1)S(1)}, bf16[3,64,128]{2,1,0:T(8,128)(2,1)S(1)}, u32[]{:S(2)}, u32[]{:S(2)}) collective-permute-start(bf16[3,64,128]{2,1,0:T(8,128)(2,1)S(1)} %get-tuple-element.24), channel_id=1, source_target_pairs={{0,1},{1,2},{2,3},{3,4},{4,5},{5,6},{6,7},{7,0},{8,9},{9,10},{10,1... | collective-permute-start | bytes 147464 | tf_op jit(solution)/shard_map/ppermute | solution.py:367
  80.0 12.6 %collective-permute-start.13 = (bf16[3,64,128]{2,1,0:T(8,128)(2,1)S(1)}, bf16[3,64,128]{2,1,0:T(8,128)(2,1)S(1)}, u32[]{:S(2)}, u32[]{:S(2)}) collective-permute-start(bf16[3,64,128]{2,1,0:T(8,128)(2,1)S(1)} %get-tuple-element.25), channel_id=1, source_target_pairs={{0,2},{1,3},{2,4},{3,5},{4,6},{5,7},{6,0},{7,1},{8,10},{9,11},{10,... | collective-permute-start | bytes 147464 | tf_op jit(solution)/shard_map/ppermute | solution.py:367
  82.3 12.4 %collective-permute-start.14 = (bf16[3,64,128]{2,1,0:T(8,128)(2,1)S(1)}, bf16[3,64,128]{2,1,0:T(8,128)(2,1)S(1)}, u32[]{:S(2)}, u32[]{:S(2)}) collective-permute-start(bf16[3,64,128]{2,1,0:T(8,128)(2,1)S(1)} %get-tuple-element.26), channel_id=1, source_target_pairs={{0,3},{1,4},{2,5},{3,6},{4,7},{5,0},{6,1},{7,2},{8,11},{9,12},{10,... | collective-permute-start | bytes 147464 | tf_op jit(solution)/shard_map/ppermute | solution.py:367
  85.3 9.4 %collective-permute-start.15 = (bf16[3,64,128]{2,1,0:T(8,128)(2,1)S(1)}, bf16[3,64,128]{2,1,0:T(8,128)(2,1)S(1)}, u32[]{:S(2)}, u32[]{:S(2)}) collective-permute-start(bf16[3,64,128]{2,1,0:T(8,128)(2,1)S(1)} %get-tuple-element.27), channel_id=1, source_target_pairs={{0,4},{1,5},{2,6},{3,7},{4,0},{5,1},{6,2},{7,3},{8,12},{9,13},{10,... | collective-permute-start | bytes 147464 | tf_op jit(solution)/shard_map/ppermute | solution.py:367
  86.2 8.7 %collective-permute-start.16 = (bf16[3,64,128]{2,1,0:T(8,128)(2,1)S(1)}, bf16[3,64,128]{2,1,0:T(8,128)(2,1)S(1)}, u32[]{:S(2)}, u32[]{:S(2)}) collective-permute-start(bf16[3,64,128]{2,1,0:T(8,128)(2,1)S(1)} %get-tuple-element.28), channel_id=1, source_target_pairs={{0,5},{1,6},{2,7},{3,0},{4,1},{5,2},{6,3},{7,4},{8,13},{9,14},{10,... | collective-permute-start | bytes 147464 | tf_op jit(solution)/shard_map/ppermute | solution.py:367
  89.9 6.6 %collective-permute-start.17 = (bf16[3,64,128]{2,1,0:T(8,128)(2,1)S(1)}, bf16[3,64,128]{2,1,0:T(8,128)(2,1)S(1)}, u32[]{:S(2)}, u32[]{:S(2)}) collective-permute-start(bf16[3,64,128]{2,1,0:T(8,128)(2,1)S(1)} %get-tuple-element.29), channel_id=1, source_target_pairs={{0,6},{1,7},{2,0},{3,1},{4,2},{5,3},{6,4},{7,5},{8,14},{9,15},{10,... | collective-permute-start | bytes 147464 | tf_op jit(solution)/shard_map/ppermute | solution.py:367
  92.6 4.4 %collective-permute-start.18 = (bf16[3,64,128]{2,1,0:T(8,128)(2,1)S(1)}, bf16[3,64,128]{2,1,0:T(8,128)(2,1)S(1)}, u32[]{:S(2)}, u32[]{:S(2)}) collective-permute-start(bf16[3,64,128]{2,1,0:T(8,128)(2,1)S(1)} %get-tuple-element.30), channel_id=1, source_target_pairs={{0,7},{1,0},{2,1},{3,2},{4,3},{5,4},{6,5},{7,6},{8,15},{9,8},{10,9... | collective-permute-start | bytes 147464 | tf_op jit(solution)/shard_map/ppermute | solution.py:367

commit v2 on v1

--- a/solution.py
+++ b/solution.py
@@ -45,20 +45,34 @@
     return (owner * nx + x) * share + n % share
 
 
-def hidden_kernel(counts, me_ref, roll_ref, starts_ref, *refs):
-    outside, lat_refs, refs = refs[:3], refs[3:5], refs[5:]
-    hid, own_ref, norm_ref, win, lhs, sums, wk_ref, wown_ref, *inside, sems = refs
-    weight_ref, gain_ref, shift_ref = inside
-    copies = [pltpu.make_async_copy(a, b, sems.at[i]) for i, (a, b) in enumerate(zip(outside, inside))]
-    for copy in copies:
-        copy.start()
-    count = counts[1]
+def prepared_kernel(counts, me_ref, roll_ref, starts_ref, weight_ref, gain_ref, shift_ref, *refs):
+    wk_ref, wown_ref, rows_ref, cached_ref = refs
+    features, own = wk_ref.shape[1], wown_ref.shape[1]
+    latents = weight_ref.shape[0] // 27
+    wk_ref[...] = jnp.zeros(wk_ref.shape, jnp.bfloat16)
+    for k in range(9):
+        for w in range(3):
+            at = k * 64 + (2 - w) * latents
+            wk_ref[at : at + latents, :] = weight_ref[(k * 3 + w) * latents : (k * 3 + w + 1) * latents, :]
+    place = lax.broadcasted_iota(jnp.int32, (features, own), 1)
+    chosen = column(place, me_ref[0], roll_ref[0], counts, own // counts[0])
+    chosen = chosen == lax.broadcasted_iota(jnp.int32, (features, own), 0)
+    chosen = jnp.where(chosen, 1.0, 0.0).astype(jnp.bfloat16)
+    wown_ref[...] = jnp.dot(wk_ref[...], chosen, preferred_element_type=jnp.float32).astype(jnp.bfloat16)
+    rows_ref[0:1, :] = gain_ref[...]
+    rows_ref[1:2, :] = shift_ref[...]
+    for s in range(starts_ref.shape[0]):
+        cached_ref[s : s + 1, :] = jnp.where(starts_ref[s] > 0, jnp.ones((1, 128), jnp.float32), 0.0)
+
+
+def hidden_kernel(count, me_ref, *refs):
+    lat_refs, refs = refs[:2], refs[2:]
+    wk_ref, wown_ref, rows_ref, cached_ref, hid, own_ref, norm_ref, win, lhs, sums = refs
     slots, total, height, lanes = lat_refs[0].shape[1:]
     frames = total - 2
     cells = count * height * 8
-    features = gain_ref.shape[1]
+    features = wk_ref.shape[1]
     own = wown_ref.shape[1]
-    latents = lanes // 8
     win[:, :, 0:8, :] = jnp.zeros((slots, total, 8, lanes), jnp.float32)
     win[:, :, cells + 8 : cells + 16, :] = jnp.zeros((slots, total, 8, lanes), jnp.float32)
     rows = total * height
@@ -75,24 +89,12 @@
         start = pl.multiple_of(8 + (me_ref[0] ^ flip) * (height * 8), 8)
         for s in range(slots):
             v = lat_refs[p * 2 // count][p % (count // 2), s].astype(jnp.float32)
-            v = jnp.where((frame > 1) | (starts_ref[s] > 0), v, 0.0).reshape(rows, 1, lanes)
+            v = jnp.where(frame > 1, v, v * cached_ref[s : s + 1, :]).reshape(rows, 1, lanes)
             v = jnp.broadcast_to(v, (rows, 8, lanes)).reshape(rows * 8, lanes)
             v = pltpu.roll(v, 0, 1, stride=16, stride_axis=0)
             v = jnp.where(keep, v, 0.0)
             v = v + pltpu.roll(v, 64, 1)
             win[s, :, pl.ds(start, height * 8), :] = v.reshape(total, height * 8, lanes)
-    wk_ref[...] = jnp.zeros(wk_ref.shape, jnp.bfloat16)
-    for copy in copies:
-        copy.wait()
-    for k in range(9):
-        for w in range(3):
-            at = k * 64 + (2 - w) * latents
-            wk_ref[at : at + latents, :] = weight_ref[(k * 3 + w) * latents : (k * 3 + w + 1) * latents, :]
-    place = lax.broadcasted_iota(jnp.int32, (features, own), 1)
-    chosen = column(place, me_ref[0], roll_ref[0], counts, own // counts[0])
-    chosen = chosen == lax.broadcasted_iota(jnp.int32, (features, own), 0)
-    chosen = jnp.where(chosen, 1.0, 0.0).astype(jnp.bfloat16)
-    wown_ref[...] = jnp.dot(wk_ref[...], chosen, preferred_element_type=jnp.float32).astype(jnp.bfloat16)
     low = lax.broadcasted_iota(jnp.int32, (cells, lanes), 1) < 64
     for s in range(slots):
         for f in range(frames):
@@ -121,9 +123,9 @@
     ) / (cells * size)
     mean = means[0:8]
     spread = means[8:16] - mean * mean
-    scale = lax.rsqrt(spread + EPSILON) * gain_ref[...]
+    scale = lax.rsqrt(spread + EPSILON) * rows_ref[0:1, :]
     norm_ref[0:8, :] = scale
-    norm_ref[8:16, :] = shift_ref[...] - mean * scale
+    norm_ref[8:16, :] = rows_ref[1:2, :] - mean * scale
 
 
 def active_kernel(hid_ref, norm_ref, act_ref):
@@ -320,10 +322,25 @@
     target = target + line // own % slots * features
     place = (target[:, None] == jnp.arange(slots * features)[None, :]).astype(bf16)
 
+    roll1 = roll.reshape(1).astype(jnp.int32)
+    prepared = call(
+        lambda *refs: prepared_kernel((nr, nx), *refs),
+        [me1, roll1, starts],
+        [entry_weight, norm_gain[None], norm_shift[None]],
+        (
+            shape((640, features), bf16),
+            shape((640, own), bf16),
+            shape((8, features), f32),
+            shape((8, widths * latents), f32),
+        ),
+        [],
+        8,
+        100_000_000,
+    )
     hid, hid_own, norm = call(
-        lambda *refs: hidden_kernel((nr, nx), *refs),
-        [me1, roll.reshape(1).astype(jnp.int32), starts],
-        [entry_weight, norm_gain[None], norm_shift[None], *lats],
+        lambda *refs: hidden_kernel(nx, *refs),
+        [me1],
+        [*lats, *prepared],
         (
             shape((slots, frames, cells, features), f32),
             shape((frames, cells, slots * own), f32),
@@ -333,16 +350,9 @@
             pltpu.VMEM((slots, frames + 2, cells + 16, widths * latents), f32),
             pltpu.VMEM((cells, 640), bf16),
             pltpu.VMEM((16, features), f32),
-            pltpu.VMEM((640, features), bf16),
-            pltpu.VMEM((640, own), bf16),
-            pltpu.VMEM(entry_weight.shape, bf16),
-            pltpu.VMEM((1, features), f32),
-            pltpu.VMEM((1, features), f32),
-            pltpu.SemaphoreType.DMA((3,)),
         ],
         24,
         5_000_000_000,
-        outside=3,
     )
     act = call(active_kernel, [], [hid, norm], shape((slots, frames, cells, features), bf16), [], 16, 3_000_000_000)
     sums = shape((slots, frames, cells + 16, 3 * own), f32)

time: 98.7 us -> 96 us (0.973)
  the two profiles are of different devices: /device:TPU:640 before, /device:TPU:516 now
where the time goes in v2:
time: 96 us; the launch traced here: 95.7 us
  starting transfers between devices  54.7 us (57%)
  Pallas kernels  19.4 us (20%)
  waiting for transfers between devices  15.1 us (16%)
  local copies, waits for them, and re-layouts  5.88 us (6%)
    pallas_call x8, Pallas kernels, call(): pl.pallas_call(kernel, out_shape=outs, in_specs=[SMEM] * len(scalars) + [...  19.4 us
    ppermute x4, starting transfers between devices, on_device(): feats[k] = from_one = lax.ppermute(to_one, 'rows', one)  16.3 us
    all_to_all x1, starting transfers between devices, on_device(): lax.all_to_all(mine, 'roll', 0, 0, axis_index_groups=same_core, tiled=True)  13.2 us
    ppermute x7, starting transfers between devices, on_device(): lax.ppermute(pieces[d], 'rows', turned[d])  13 us
    ppermute x3, starting transfers between devices, on_device(): came = lax.ppermute(lat, 'rows', [(i, i ^ bit) for i in range(nx)])  9.75 us
    ppermute x7, waiting for transfers between devices, on_device(): lax.ppermute(pieces[d], 'rows', turned[d])  5.55 us
    all_to_all x1, waiting for transfers between devices, on_device(): lax.all_to_all(mine, 'roll', 0, 0, axis_index_groups=same_core, tiled=True)  5.35 us
    unnamed x18, local copies, waits for them, and re-layouts  3.77 us
  transfers between devices with their start and end apart: 20, of which 5 were waited for; matrix products, arithmetic and copies ran while one was open for 0% of the time, Pallas kernels for 15%

profile of v2, /device:TPU:516, one launch (start us, length us, event | category | flops | bytes accessed | tf_op | source)
XLA Modules:
  0.0 95.7 jit_solution(16232534574498548202)
XLA Ops:
  0.0 2.1 %broadcast_in_dim.16 = bf16[8,4,13824]{2,1,0:T(4,128)(2,1)} broadcast(bf16[4,13824]{1,0:T(4,128)(2,1)} %bitcast.12), dimensions={1,2} | broadcast | bytes 995328 | tf_op jit(solution)/shard_map/broadcast_in_dim | solution.py:316
  2.1 13.2 %all-to-all-start = ((bf16[8,4,13824]{2,1,0:T(4,128)(2,1)}), bf16[8,4,13824]{2,1,0:T(4,128)(2,1)S(1)}, u32[]{:S(2)}, u32[]{:S(2)}) async-start(bf16[8,4,13824]{2,1,0:T(4,128)(2,1)} %broadcast_in_dim.16), calls=%async_computation | async-start | bytes 1769472 | tf_op jit(solution)/shard_map/all_to_all | solution.py:317
  15.3 0.9 copy-done.1
  16.2 0.8 copy-done.2
  17.0 0.4 shard_map.100
  17.4 4.4 %collective-permute-start.8 = (bf16[1,2,5,8,128]{4,3,2,1,0:T(8,128)(2,1)S(1)}, bf16[1,2,5,8,128]{4,3,2,1,0:T(8,128)(2,1)S(1)}, u32[]{:S(2)}, u32[]{:S(2)}) collective-permute-start(bf16[1,2,5,8,128]{4,3,2,1,0:T(8,128)(2,1)S(1)} %shard_map.100), channel_id=1, source_target_pairs={{0,4},{1,5},{2,6},{3,7},{4,0},{5,1},{6,2},{7,3},{8,12},{9,13},{10,... | collective-permute-start | bytes 61448 | tf_op jit(solution)/shard_map/ppermute | solution.py:295
  21.8 1.3 %collective-permute-start.1 = (bf16[2,2,64,512]{3,2,1,0:T(8,128)(2,1)}, bf16[2,2,64,512]{3,2,1,0:T(8,128)(2,1)S(1)}, u32[]{:S(2)}, u32[]{:S(2)}) collective-permute-start(bf16[2,2,64,512]{3,2,1,0:T(8,128)(2,1)} %bitcast.9), channel_id=1, source_target_pairs={{0,7},{1,2},{2,1},{3,4},{4,3},{5,6},{6,5},{7,0},{8,15},{9,10},{10,... | collective-permute-start | bytes 786440 | tf_op jit(solution)/shard_map/ppermute | solution.py:311
  23.1 8.4 %collective-permute-start = (bf16[2,2,64,512]{3,2,1,0:T(8,128)(2,1)}, bf16[2,2,64,512]{3,2,1,0:T(8,128)(2,1)S(1)}, u32[]{:S(2)}, u32[]{:S(2)}) collective-permute-start(bf16[2,2,64,512]{3,2,1,0:T(8,128)(2,1)} %bitcast.10), channel_id=1, source_target_pairs={{0,1},{1,0},{2,3},{3,2},{4,5},{5,4},{6,7},{7,6},{8,9},{9,8},{10,11... | collective-permute-start | bytes 786440 | tf_op jit(solution)/shard_map/ppermute | solution.py:310
  31.5 0.0 collective-permute-done.8
  31.5 3.7 %collective-permute-start.9 = (bf16[2,2,5,8,128]{4,3,2,1,0:T(8,128)(2,1)S(1)}, bf16[2,2,5,8,128]{4,3,2,1,0:T(8,128)(2,1)S(1)}, u32[]{:S(2)}, u32[]{:S(2)}) collective-permute-start(bf16[2,2,5,8,128]{4,3,2,1,0:T(8,128)(2,1)S(1)} %pad_maximum_fusion.1), channel_id=1, source_target_pairs={{0,2},{1,3},{2,0},{3,1},{4,6},{5,7},{6,4},{7,5},{8,10},{9,11},{10,... | collective-permute-start | bytes 122888 | tf_op jit(solution)/shard_map/ppermute | solution.py:295
  35.2 5.4 %all-to-all-done.mine_ref = bf16[8,4,13824]{2,1,0:T(4,128)(2,1)S(1)} async-done(((bf16[8,4,13824]{2,1,0:T(4,128)(2,1)}), bf16[8,4,13824]{2,1,0:T(4,128)(2,1)S(1)}, u32[]{:S(2)}, u32[]{:S(2)}) %all-to-all-start) | async-done | bytes 884768 | tf_op jit(solution)/shard_map/all_to_all | solution.py:317
  40.5 0.0 collective-permute-start.11
  40.6 0.0 collective-permute-done.9
  40.6 1.7 %collective-permute-start.10 = (bf16[4,2,5,8,128]{4,3,2,1,0:T(8,128)(2,1)S(1)}, bf16[4,2,5,8,128]{4,3,2,1,0:T(8,128)(2,1)S(1)}, u32[]{:S(2)}, u32[]{:S(2)}) collective-permute-start(bf16[4,2,5,8,128]{4,3,2,1,0:T(8,128)(2,1)S(1)} %pad_maximum_fusion.refs_1_), channel_id=1, source_target_pairs={{0,1},{1,0},{2,3},{3,2},{4,5},{5,4},{6,7},{7,6},{8,9},{9,8},{10,11... | collective-permute-start | bytes 245768 | tf_op jit(solution)/shard_map/ppermute | solution.py:295
  42.3 0.7 copy-done.3
  43.0 0.7 copy-done.4
  43.7 0.7 copy-done.5
  44.4 0.9 shard_map.101
  45.3 0.5 collective-permute-start.2
  45.8 0.0 collective-permute-done.refs_5_
  45.8 0.4 collective-permute-start.3
  46.2 0.0 collective-permute-done.10.refs_2_
  46.2 6.0 %shard_map.102 = (f32[2,3,512,512]{3,2,1,0:T(8,128)S(1)}, f32[3,512,128]{2,1,0:T(8,128)S(1)}, f32[16,512]{1,0:T(8,128)S(1)}) custom-call(s32[1]{0:T(128)} %bitcast.refs_0_, bf16[4,2,5,8,128]{4,3,2,1,0:T(8,128)(2,1)S(1)} %pad_maximum_fusion.refs_1_, bf16[4,2,5,8,128]{4,3,2,1,0:T(8,128)(2,1)S(1)} %collective-permute-done.10.refs_2_, ...), custom_call_target="tpu_custom_call" | custom-call | flops 5000000000 | bytes 4194304 | tf_op jit(solution)/shard_map/pallas_call | solution.py:240
  52.2 1.6 %collective-permute-done.2.refs_6_ = bf16[2,2,64,512]{3,2,1,0:T(8,128)(2,1)S(1)} collective-permute-done((bf16[2,2,64,512]{3,2,1,0:T(8,128)(2,1)S(1)}, bf16[2,2,64,512]{3,2,1,0:T(8,128)(2,1)S(1)}, u32[]{:S(2)}, u32[]{:S(2)}) %collective-permute-start.2) | collective-permute-done | bytes 262176 | tf_op jit(solution)/shard_map/ppermute | solution.py:310
  53.8 0.5 collective-permute-start.5
  54.3 0.0 collective-permute-done.3.refs_10_
  54.3 3.1 %collective-permute-start.4 = (bf16[2,2,64,512]{3,2,1,0:T(8,128)(2,1)S(1)}, bf16[2,2,64,512]{3,2,1,0:T(8,128)(2,1)S(1)}, u32[]{:S(2)}, u32[]{:S(2)}) collective-permute-start(bf16[2,2,64,512]{3,2,1,0:T(8,128)(2,1)S(1)} %collective-permute-done.3.refs_10_), channel_id=1, source_target_pairs={{0,1},{1,0},{2,3},{3,2},{4,5},{5,4},{6,7},{7,6},{8,9},{9,8},{10,11... | collective-permute-start | bytes 786440 | tf_op jit(solution)/shard_map/ppermute | solution.py:310
  57.4 1.4 %shard_map.103.act_ref = bf16[2,3,512,512]{3,2,1,0:T(8,128)(2,1)S(1)} custom-call(f32[2,3,512,512]{3,2,1,0:T(8,128)S(1)} %get-tuple-element.26.hid_ref, f32[16,512]{1,0:T(8,128)S(1)} %get-tuple-element.27.norm_ref), custom_call_target="tpu_custom_call" | custom-call | flops 3000000000 | bytes 4194304 | tf_op jit(solution)/shard_map/pallas_call | solution.py:240
  58.8 2.6 %collective-permute-done.5.refs_9_ = bf16[2,2,64,512]{3,2,1,0:T(8,128)(2,1)S(1)} collective-permute-done((bf16[2,2,64,512]{3,2,1,0:T(8,128)(2,1)S(1)}, bf16[2,2,64,512]{3,2,1,0:T(8,128)(2,1)S(1)}, u32[]{:S(2)}, u32[]{:S(2)}) %collective-permute-start.5) | collective-permute-done | bytes 262176 | tf_op jit(solution)/shard_map/ppermute | solution.py:311
  61.4 4.3 %collective-permute-start.6 = (bf16[1,2,64,512]{3,2,1,0:T(8,128)(2,1)S(1)}, bf16[1,2,64,512]{3,2,1,0:T(8,128)(2,1)S(1)}, u32[]{:S(2)}, u32[]{:S(2)}) collective-permute-start(bf16[1,2,64,512]{3,2,1,0:T(8,128)(2,1)S(1)} %slice.8), channel_id=1, source_target_pairs={{0,1},{1,0},{2,3},{3,2},{4,5},{5,4},{6,7},{7,6},{8,9},{9,8},{10,11... | collective-permute-start | bytes 393224 | tf_op jit(solution)/shard_map/ppermute | solution.py:310
  65.7 0.0 collective-permute-done.4.refs_7_
  65.7 0.3 collective-permute-start.7
  65.9 2.8 %shard_map.104 = (f32[2,3,528,192]{3,2,1,0:T(8,128)S(1)}, bf16[64,13824]{1,0:T(8,128)(2,1)S(1)}) custom-call(bf16[2,3,512,512]{3,2,1,0:T(8,128)(2,1)S(1)} %shard_map.103.act_ref, bf16[8,4,13824]{2,1,0:T(4,128)(2,1)S(1)} %all-to-all-done.mine_ref, bf16[8,4,13824]{2,1,0:T(4,128)(2,1)S(1)} %collective-permute-done.11.other_ref), custom_call_target="tpu_custom_call" | custom-call | flops 3000000000 | bytes 4194304 | tf_op jit(solution)/shard_map/pallas_call | solution.py:240
  68.8 0.0 copy-start.6
  68.8 0.0 copy-start.7
  68.8 0.0 copy-start.8
  68.8 2.6 %shard_map.105.refs_15_ = f32[2,3,528,192]{3,2,1,0:T(8,128)S(1)} custom-call(bf16[2,3,512,512]{3,2,1,0:T(8,128)(2,1)S(1)} %shard_map.103.act_ref, bf16[64,13824]{1,0:T(8,128)(2,1)S(1)} %get-tuple-element.28.w_ref.refs_13_, f32[2,3,528,192]{3,2,1,0:T(8,128)S(1)} %get-tuple-element.30._), custom_call_target="tpu_custom_call", output_to_operand_aliasing={{}: (2, {})} | custom-call | flops 3000000000 | bytes 4194304 | tf_op jit(solution)/shard_map/pallas_call | solution.py:240
  71.5 3.8 %shard_map.106 = (bf16[3,64,128]{2,1,0:T(8,128)(2,1)S(1)}, bf16[3,64,128]{2,1,0:T(8,128)(2,1)S(1)}, bf16[3,64,128]{2,1,0:T(8,128)(2,1)S(1)}, bf16[3,64,128]{2,1,...) custom-call(s32[1]{0:T(128)} %bitcast.refs_0_, ...), custom_call_target="tpu_custom_call", output_to_operand_aliasing={{8}: (15, {})} | custom-call | flops 3000000000 | bytes 4194304 | tf_op jit(solution)/shard_map/pallas_call | solution.py:240
  75.4 1.6 %collective-permute-start.12 = (bf16[3,64,128]{2,1,0:T(8,128)(2,1)S(1)}, bf16[3,64,128]{2,1,0:T(8,128)(2,1)S(1)}, u32[]{:S(2)}, u32[]{:S(2)}) collective-permute-start(bf16[3,64,128]{2,1,0:T(8,128)(2,1)S(1)} %get-tuple-element.32), channel_id=1, source_target_pairs={{0,1},{1,2},{2,3},{3,4},{4,5},{5,6},{6,7},{7,0},{8,9},{9,10},{10,1... | collective-permute-start | bytes 147464 | tf_op jit(solution)/shard_map/ppermute | solution.py:377
  76.9 1.2 %collective-permute-start.13 = (bf16[3,64,128]{2,1,0:T(8,128)(2,1)S(1)}, bf16[3,64,128]{2,1,0:T(8,128)(2,1)S(1)}, u32[]{:S(2)}, u32[]{:S(2)}) collective-permute-start(bf16[3,64,128]{2,1,0:T(8,128)(2,1)S(1)} %get-tuple-element.33), channel_id=1, source_target_pairs={{0,2},{1,3},{2,4},{3,5},{4,6},{5,7},{6,0},{7,1},{8,10},{9,11},{10,... | collective-permute-start | bytes 147464 | tf_op jit(solution)/shard_map/ppermute | solution.py:377
  78.2 2.6 %collective-permute-start.14 = (bf16[3,64,128]{2,1,0:T(8,128)(2,1)S(1)}, bf16[3,64,128]{2,1,0:T(8,128)(2,1)S(1)}, u32[]{:S(2)}, u32[]{:S(2)}) collective-permute-start(bf16[3,64,128]{2,1,0:T(8,128)(2,1)S(1)} %get-tuple-element.34), channel_id=1, source_target_pairs={{0,3},{1,4},{2,5},{3,6},{4,7},{5,0},{6,1},{7,2},{8,11},{9,12},{10,... | collective-permute-start | bytes 147464 | tf_op jit(solution)/shard_map/ppermute | solution.py:377
  80.8 3.9 %collective-permute-start.15 = (bf16[3,64,128]{2,1,0:T(8,128)(2,1)S(1)}, bf16[3,64,128]{2,1,0:T(8,128)(2,1)S(1)}, u32[]{:S(2)}, u32[]{:S(2)}) collective-permute-start(bf16[3,64,128]{2,1,0:T(8,128)(2,1)S(1)} %get-tuple-element.35), channel_id=1, source_target_pairs={{0,4},{1,5},{2,6},{3,7},{4,0},{5,1},{6,2},{7,3},{8,12},{9,13},{10,... | collective-permute-start | bytes 147464 | tf_op jit(solution)/shard_map/ppermute | solution.py:377
  84.7 2.9 %collective-permute-start.16 = (bf16[3,64,128]{2,1,0:T(8,128)(2,1)S(1)}, bf16[3,64,128]{2,1,0:T(8,128)(2,1)S(1)}, u32[]{:S(2)}, u32[]{:S(2)}) collective-permute-start(bf16[3,64,128]{2,1,0:T(8,128)(2,1)S(1)} %get-tuple-element.36), channel_id=1, source_target_pairs={{0,5},{1,6},{2,7},{3,0},{4,1},{5,2},{6,3},{7,4},{8,13},{9,14},{10,... | collective-permute-start | bytes 147464 | tf_op jit(solution)/shard_map/ppermute | solution.py:377
  87.6 0.9 collective-permute-start.18
  88.4 0.4 fusion.refs_8_
  88.9 3.5 %collective-permute-done.16.refs_5_ = bf16[3,64,128]{2,1,0:T(8,128)(2,1)S(1)} collective-permute-done((bf16[3,64,128]{2,1,0:T(8,128)(2,1)S(1)}, bf16[3,64,128]{2,1,0:T(8,128)(2,1)S(1)}, u32[]{:S(2)}, u32[]{:S(2)}) %collective-permute-start.16) | collective-permute-done | bytes 49184 | tf_op jit(solution)/shard_map/ppermute | solution.py:377
  92.3 2.1 %collective-permute-done.17.refs_6_ = bf16[3,64,128]{2,1,0:T(8,128)(2,1)S(1)} collective-permute-done((bf16[3,64,128]{2,1,0:T(8,128)(2,1)S(1)}, bf16[3,64,128]{2,1,0:T(8,128)(2,1)S(1)}, u32[]{:S(2)}, u32[]{:S(2)}) %collective-permute-start.17) | collective-permute-done | bytes 49184 | tf_op jit(solution)/shard_map/ppermute | solution.py:377
  94.4 1.3 %shard_map.107 = bf16[2,192,512]{2,1,0:T(8,128)(2,1)} custom-call(bf16[3,64,128]{2,1,0:T(8,128)(2,1)S(1)} %get-tuple-element.31.refs_0_, bf16[3,64,128]{2,1,0:T(8,128)(2,1)S(1)} %collective-permute-done.12.refs_1_, bf16[3,64,128]{2,1,0:T(8,128)(2,1)S(1)} %collective-permute-done.13.refs_2_, bf16[3,64,128]{2,1,0:T(8,128)(2,1)S(1)} %collective-permute-done.14.refs_3_, ...), custom_call_target="tpu_custom_call" | custom-call | flops 400000000 | bytes 4194304 | tf_op jit(solution)/shard_map/pallas_call | solution.py:240
  (25 shorter events, 0.1 us)
Async XLA Ops:
  0.0 42.3 %copy-start = (bf16[432,512]{1,0:T(8,128)(2,1)S(1)}, bf16[432,512]{1,0:T(8,128)(2,1)}, u32[]{:S(2)}) copy-start(bf16[432,512]{1,0:T(8,128)(2,1)} %refs_3_.2) | copy-start | bytes 1327108
  2.1 38.4 %all-to-all-start = ((bf16[8,4,13824]{2,1,0:T(4,128)(2,1)}), bf16[8,4,13824]{2,1,0:T(4,128)(2,1)S(1)}, u32[]{:S(2)}, u32[]{:S(2)}) async-start(bf16[8,4,13824]{2,1,0:T(4,128)(2,1)} %broadcast_in_dim.16), calls=%async_computation | async-start | bytes 1769472 | tf_op jit(solution)/shard_map/all_to_all | solution.py:317
  15.3 0.9 copy-start.1
  16.2 0.8 copy-start.2
  17.4 14.1 %collective-permute-start.8 = (bf16[1,2,5,8,128]{4,3,2,1,0:T(8,128)(2,1)S(1)}, bf16[1,2,5,8,128]{4,3,2,1,0:T(8,128)(2,1)S(1)}, u32[]{:S(2)}, u32[]{:S(2)}) collective-permute-start(bf16[1,2,5,8,128]{4,3,2,1,0:T(8,128)(2,1)S(1)} %shard_map.100), channel_id=1, source_target_pairs={{0,4},{1,5},{2,6},{3,7},{4,0},{5,1},{6,2},{7,3},{8,12},{9,13},{10,... | collective-permute-start | bytes 61448 | tf_op jit(solution)/shard_map/ppermute | solution.py:295
  21.8 23.5 %collective-permute-start.1 = (bf16[2,2,64,512]{3,2,1,0:T(8,128)(2,1)}, bf16[2,2,64,512]{3,2,1,0:T(8,128)(2,1)S(1)}, u32[]{:S(2)}, u32[]{:S(2)}) collective-permute-start(bf16[2,2,64,512]{3,2,1,0:T(8,128)(2,1)} %bitcast.9), channel_id=1, source_target_pairs={{0,7},{1,2},{2,1},{3,4},{4,3},{5,6},{6,5},{7,0},{8,15},{9,10},{10,... | collective-permute-start | bytes 786440 | tf_op jit(solution)/shard_map/ppermute | solution.py:311
  23.1 22.7 %collective-permute-start = (bf16[2,2,64,512]{3,2,1,0:T(8,128)(2,1)}, bf16[2,2,64,512]{3,2,1,0:T(8,128)(2,1)S(1)}, u32[]{:S(2)}, u32[]{:S(2)}) collective-permute-start(bf16[2,2,64,512]{3,2,1,0:T(8,128)(2,1)} %bitcast.10), channel_id=1, source_target_pairs={{0,1},{1,0},{2,3},{3,2},{4,5},{5,4},{6,7},{7,6},{8,9},{9,8},{10,11... | collective-permute-start | bytes 786440 | tf_op jit(solution)/shard_map/ppermute | solution.py:310
  31.5 9.0 %collective-permute-start.9 = (bf16[2,2,5,8,128]{4,3,2,1,0:T(8,128)(2,1)S(1)}, bf16[2,2,5,8,128]{4,3,2,1,0:T(8,128)(2,1)S(1)}, u32[]{:S(2)}, u32[]{:S(2)}) collective-permute-start(bf16[2,2,5,8,128]{4,3,2,1,0:T(8,128)(2,1)S(1)} %pad_maximum_fusion.1), channel_id=1, source_target_pairs={{0,2},{1,3},{2,0},{3,1},{4,6},{5,7},{6,4},{7,5},{8,10},{9,11},{10,... | collective-permute-start | bytes 122888 | tf_op jit(solution)/shard_map/ppermute | solution.py:295
  40.5 25.4 %collective-permute-start.11 = (bf16[8,4,13824]{2,1,0:T(4,128)(2,1)S(1)}, bf16[8,4,13824]{2,1,0:T(4,128)(2,1)S(1)}, u32[]{:S(2)}, u32[]{:S(2)}) collective-permute-start(bf16[8,4,13824]{2,1,0:T(4,128)(2,1)S(1)} %all-to-all-done.mine_ref), channel_id=1, source_target_pairs={{0,8},{8,0},{16,24},{24,16},{32,40},{40,32},{48,56},{56,48},{64,72... | collective-permute-start | bytes 2654216 | tf_op jit(solution)/shard_map/ppermute | solution.py:318
  40.6 5.6 %collective-permute-start.10 = (bf16[4,2,5,8,128]{4,3,2,1,0:T(8,128)(2,1)S(1)}, bf16[4,2,5,8,128]{4,3,2,1,0:T(8,128)(2,1)S(1)}, u32[]{:S(2)}, u32[]{:S(2)}) collective-permute-start(bf16[4,2,5,8,128]{4,3,2,1,0:T(8,128)(2,1)S(1)} %pad_maximum_fusion.refs_1_), channel_id=1, source_target_pairs={{0,1},{1,0},{2,3},{3,2},{4,5},{5,4},{6,7},{7,6},{8,9},{9,8},{10,11... | collective-permute-start | bytes 245768 | tf_op jit(solution)/shard_map/ppermute | solution.py:295
  42.3 0.7 copy-start.3
  43.0 0.7 copy-start.4
  43.7 0.7 copy-start.5
  45.3 8.5 %collective-permute-start.2 = (bf16[2,2,64,512]{3,2,1,0:T(8,128)(2,1)S(1)}, bf16[2,2,64,512]{3,2,1,0:T(8,128)(2,1)S(1)}, u32[]{:S(2)}, u32[]{:S(2)}) collective-permute-start(bf16[2,2,64,512]{3,2,1,0:T(8,128)(2,1)S(1)} %collective-permute-done.1.refs_11_), channel_id=1, source_target_pairs={{0,1},{1,0},{2,3},{3,2},{4,5},{5,4},{6,7},{7,6},{8,9},{9,8},{10,11... | collective-permute-start | bytes 786440 | tf_op jit(solution)/shard_map/ppermute | solution.py:310
  45.8 8.5 %collective-permute-start.3 = (bf16[2,2,64,512]{3,2,1,0:T(8,128)(2,1)S(1)}, bf16[2,2,64,512]{3,2,1,0:T(8,128)(2,1)S(1)}, u32[]{:S(2)}, u32[]{:S(2)}) collective-permute-start(bf16[2,2,64,512]{3,2,1,0:T(8,128)(2,1)S(1)} %collective-permute-done.refs_5_), channel_id=1, source_target_pairs={{0,7},{1,2},{2,1},{3,4},{4,3},{5,6},{6,5},{7,0},{8,15},{9,10},{10,... | collective-permute-start | bytes 786440 | tf_op jit(solution)/shard_map/ppermute | solution.py:311
  53.8 7.6 %collective-permute-start.5 = (bf16[2,2,64,512]{3,2,1,0:T(8,128)(2,1)S(1)}, bf16[2,2,64,512]{3,2,1,0:T(8,128)(2,1)S(1)}, u32[]{:S(2)}, u32[]{:S(2)}) collective-permute-start(bf16[2,2,64,512]{3,2,1,0:T(8,128)(2,1)S(1)} %collective-permute-done.2.refs_6_), channel_id=1, source_target_pairs={{0,7},{1,2},{2,1},{3,4},{4,3},{5,6},{6,5},{7,0},{8,15},{9,10},{10,... | collective-permute-start | bytes 786440 | tf_op jit(solution)/shard_map/ppermute | solution.py:311
  54.3 11.4 %collective-permute-start.4 = (bf16[2,2,64,512]{3,2,1,0:T(8,128)(2,1)S(1)}, bf16[2,2,64,512]{3,2,1,0:T(8,128)(2,1)S(1)}, u32[]{:S(2)}, u32[]{:S(2)}) collective-permute-start(bf16[2,2,64,512]{3,2,1,0:T(8,128)(2,1)S(1)} %collective-permute-done.3.refs_10_), channel_id=1, source_target_pairs={{0,1},{1,0},{2,3},{3,2},{4,5},{5,4},{6,7},{7,6},{8,9},{9,8},{10,11... | collective-permute-start | bytes 786440 | tf_op jit(solution)/shard_map/ppermute | solution.py:310
  61.4 10.1 %collective-permute-start.6 = (bf16[1,2,64,512]{3,2,1,0:T(8,128)(2,1)S(1)}, bf16[1,2,64,512]{3,2,1,0:T(8,128)(2,1)S(1)}, u32[]{:S(2)}, u32[]{:S(2)}) collective-permute-start(bf16[1,2,64,512]{3,2,1,0:T(8,128)(2,1)S(1)} %slice.8), channel_id=1, source_target_pairs={{0,1},{1,0},{2,3},{3,2},{4,5},{5,4},{6,7},{7,6},{8,9},{9,8},{10,11... | collective-permute-start | bytes 393224 | tf_op jit(solution)/shard_map/ppermute | solution.py:310
  65.7 5.8 %collective-permute-start.7 = (bf16[1,2,64,512]{3,2,1,0:T(8,128)(2,1)S(1)}, bf16[1,2,64,512]{3,2,1,0:T(8,128)(2,1)S(1)}, u32[]{:S(2)}, u32[]{:S(2)}) collective-permute-start(bf16[1,2,64,512]{3,2,1,0:T(8,128)(2,1)S(1)} %slice.9), channel_id=1, source_target_pairs={{0,7},{1,2},{2,1},{3,4},{4,3},{5,6},{6,5},{7,0},{8,15},{9,10},{10,... | collective-permute-start | bytes 393224 | tf_op jit(solution)/shard_map/ppermute | solution.py:311
  68.8 2.7 %copy-start.6 = (bf16[2,2,8,8,512]{4,3,2,1,0:T(8,128)(2,1)S(1)}, bf16[2,2,8,8,512]{4,3,2,1,0:T(8,128)(2,1)}, u32[]{:S(2)}) copy-start(bf16[2,2,8,8,512]{4,3,2,1,0:T(8,128)(2,1)} %param.12) | copy-start | bytes 786436
  68.8 2.7 %copy-start.7 = (s32[2]{0:T(128)S(1)}, s32[2]{0:T(128)}, u32[]{:S(2)}) copy-start(s32[2]{0:T(128)} %refs_2_.3) | copy-start | bytes 28
  68.8 2.7 %copy-start.8 = (s32[2]{0:T(128)S(1)}, s32[2]{0:T(128)}, u32[]{:S(2)}) copy-start(s32[2]{0:T(128)} %refs_3_.3) | copy-start | bytes 28
  75.4 12.2 %collective-permute-start.12 = (bf16[3,64,128]{2,1,0:T(8,128)(2,1)S(1)}, bf16[3,64,128]{2,1,0:T(8,128)(2,1)S(1)}, u32[]{:S(2)}, u32[]{:S(2)}) collective-permute-start(bf16[3,64,128]{2,1,0:T(8,128)(2,1)S(1)} %get-tuple-element.32), channel_id=1, source_target_pairs={{0,1},{1,2},{2,3},{3,4},{4,5},{5,6},{6,7},{7,0},{8,9},{9,10},{10,1... | collective-permute-start | bytes 147464 | tf_op jit(solution)/shard_map/ppermute | solution.py:377
  76.9 10.6 %collective-permute-start.13 = (bf16[3,64,128]{2,1,0:T(8,128)(2,1)S(1)}, bf16[3,64,128]{2,1,0:T(8,128)(2,1)S(1)}, u32[]{:S(2)}, u32[]{:S(2)}) collective-permute-start(bf16[3,64,128]{2,1,0:T(8,128)(2,1)S(1)} %get-tuple-element.33), channel_id=1, source_target_pairs={{0,2},{1,3},{2,4},{3,5},{4,6},{5,7},{6,0},{7,1},{8,10},{9,11},{10,... | collective-permute-start | bytes 147464 | tf_op jit(solution)/shard_map/ppermute | solution.py:377
  78.2 10.6 %collective-permute-start.14 = (bf16[3,64,128]{2,1,0:T(8,128)(2,1)S(1)}, bf16[3,64,128]{2,1,0:T(8,128)(2,1)S(1)}, u32[]{:S(2)}, u32[]{:S(2)}) collective-permute-start(bf16[3,64,128]{2,1,0:T(8,128)(2,1)S(1)} %get-tuple-element.34), channel_id=1, source_target_pairs={{0,3},{1,4},{2,5},{3,6},{4,7},{5,0},{6,1},{7,2},{8,11},{9,12},{10,... | collective-permute-start | bytes 147464 | tf_op jit(solution)/shard_map/ppermute | solution.py:377
  80.8 8.1 %collective-permute-start.15 = (bf16[3,64,128]{2,1,0:T(8,128)(2,1)S(1)}, bf16[3,64,128]{2,1,0:T(8,128)(2,1)S(1)}, u32[]{:S(2)}, u32[]{:S(2)}) collective-permute-start(bf16[3,64,128]{2,1,0:T(8,128)(2,1)S(1)} %get-tuple-element.35), channel_id=1, source_target_pairs={{0,4},{1,5},{2,6},{3,7},{4,0},{5,1},{6,2},{7,3},{8,12},{9,13},{10,... | collective-permute-start | bytes 147464 | tf_op jit(solution)/shard_map/ppermute | solution.py:377
  84.7 7.7 %collective-permute-start.16 = (bf16[3,64,128]{2,1,0:T(8,128)(2,1)S(1)}, bf16[3,64,128]{2,1,0:T(8,128)(2,1)S(1)}, u32[]{:S(2)}, u32[]{:S(2)}) collective-permute-start(bf16[3,64,128]{2,1,0:T(8,128)(2,1)S(1)} %get-tuple-element.36), channel_id=1, source_target_pairs={{0,5},{1,6},{2,7},{3,0},{4,1},{5,2},{6,3},{7,4},{8,13},{9,14},{10,... | collective-permute-start | bytes 147464 | tf_op jit(solution)/shard_map/ppermute | solution.py:377
  87.5 6.8 %collective-permute-start.17 = (bf16[3,64,128]{2,1,0:T(8,128)(2,1)S(1)}, bf16[3,64,128]{2,1,0:T(8,128)(2,1)S(1)}, u32[]{:S(2)}, u32[]{:S(2)}) collective-permute-start(bf16[3,64,128]{2,1,0:T(8,128)(2,1)S(1)} %get-tuple-element.37), channel_id=1, source_target_pairs={{0,6},{1,7},{2,0},{3,1},{4,2},{5,3},{6,4},{7,5},{8,14},{9,15},{10,... | collective-permute-start | bytes 147464 | tf_op jit(solution)/shard_map/ppermute | solution.py:377
  87.6 6.8 %collective-permute-start.18 = (bf16[3,64,128]{2,1,0:T(8,128)(2,1)S(1)}, bf16[3,64,128]{2,1,0:T(8,128)(2,1)S(1)}, u32[]{:S(2)}, u32[]{:S(2)}) collective-permute-start(bf16[3,64,128]{2,1,0:T(8,128)(2,1)S(1)} %get-tuple-element.38), channel_id=1, source_target_pairs={{0,7},{1,0},{2,1},{3,2},{4,3},{5,4},{6,5},{7,6},{8,15},{9,8},{10,9... | collective-permute-start | bytes 147464 | tf_op jit(solution)/shard_map/ppermute | solution.py:377

commit v3 on v2

--- a/solution.py
+++ b/solution.py
@@ -175,26 +175,24 @@
     new_frames((1, 0), act_ref, w_ref, acc_ref)
 
 
-def old_frames_kernel(count, me_ref, starts_ref, lengths_ref, plan_ref, *refs):
-    feat_refs = refs[: count + 1]
-    w_ref, own_ref, _ = refs[count + 1 : count + 4]
-    out_refs = refs[count + 4 : 2 * count + 4]
-    acc, feats, done = refs[2 * count + 4 :]
+def near_features_kernel(count, me_ref, starts_ref, *refs):
+    feat_refs = refs[: count - 1]
+    w_ref, _, acc, feats = refs[count - 1 :]
     slots, frames, padded_cells, _ = acc.shape
-    own = w_ref.shape[0]
     cells = padded_cells - 16
     part = cells // count
     me = me_ref[0]
     toward = 1 - 2 * lax.rem(me, 2)
     for s in range(slots):
         for d in range(count):
-            if d == count // 2:
-                v = feat_refs[d if s < slots // 2 else count][s % (slots // 2)]
-            else:
-                v = feat_refs[d][s]
             xp = lax.rem(me + toward * d + count, count)
             start = pl.multiple_of(xp * part, part)
-            feats[s, :, pl.ds(start, part), :] = jnp.where(starts_ref[s] > 0, v, jnp.zeros_like(v))
+            if d == count // 2:
+                v = jnp.zeros((2, part, feats.shape[3]), feats.dtype)
+            else:
+                v = feat_refs[d - (d > count // 2)][s]
+                v = jnp.where(starts_ref[s] > 0, v, jnp.zeros_like(v))
+            feats[s, :, pl.ds(start, part), :] = v
     for t in range(2):
         for h in range(3):
             at = (2 - h) * 8
@@ -203,6 +201,30 @@
                 for f in range(frames):
                     if f + t < 2:
                         acc[s, f, at : at + cells, :] += nt_dot(feats[s, f + t], taps)
+
+
+def far_features_kernel(count, me_ref, starts_ref, lengths_ref, plan_ref, *refs):
+    far_refs, (w_ref, own_ref, _) = refs[:2], refs[2:5]
+    out_refs = refs[5 : count + 5]
+    acc, done = refs[count + 5 :]
+    slots, frames, padded_cells, _ = acc.shape
+    own = w_ref.shape[0]
+    cells = padded_cells - 16
+    part = cells // count
+    me = me_ref[0]
+    far = []
+    for s in range(slots):
+        v = far_refs[s // (slots // 2)][s % (slots // 2)]
+        far.append(jnp.where(starts_ref[s] > 0, v, jnp.zeros_like(v)))
+    for t in range(2):
+        for h in range(3):
+            start = lax.rem(me + count // 2, count) * part + (2 - h) * 8
+            rows = pl.ds(pl.multiple_of(start, 8), part)
+            taps = taps_of(w_ref, t, h)
+            for s in range(slots):
+                for f in range(frames):
+                    if f + t < 2:
+                        acc[s, f, rows, :] += nt_dot(far[s][f + t], taps)
     col = lax.broadcasted_iota(jnp.int32, (cells // 8, 8, own), 1)
     for f in range(frames):
         parts = []
@@ -360,19 +382,27 @@
         first_offset_kernel, [], [act, mine, other], (sums, shape((own, wt.shape[1]), bf16)), [], 20, 3_000_000_000
     )
     acc = call(more_offsets_kernel, [], [act, weights, acc], sums, [], 20, 3_000_000_000, {2: 0})
+    near = [feats[d] for d in range(nx) if d != nx // 2]
+    acc = call(
+        lambda *refs: near_features_kernel(nx, *refs),
+        [me1, starts],
+        near + [weights, acc],
+        sums,
+        [pltpu.VMEM((slots, 2, cells, features), bf16)],
+        30,
+        3_000_000_000,
+        {2 + nx: 0},
+    )
     piece = shape((frames, part, slots * own), bf16)
     *pieces, _ = call(
-        lambda *refs: old_frames_kernel(nx, *refs),
+        lambda *refs: far_features_kernel(nx, *refs),
         [me1, starts, lengths, move_plan],
-        feats + [weights, hid_own, acc],
+        [feats[nx // 2], feats[nx], weights, hid_own, acc],
         (piece,) * nx + (sums,),
-        [
-            pltpu.VMEM((slots, 2, cells, features), bf16),
-            pltpu.VMEM((frames, cells, slots * own), bf16),
-        ],
-        30,
-        3_000_000_000,
-        {4 + nx + 3: nx},
+        [pltpu.VMEM((frames, cells, slots * own), bf16)],
+        20,
+        1_000_000_000,
+        {8: nx},
     )
     got = [pieces[0]] + [lax.ppermute(pieces[d], "rows", turned[d]) for d in range(1, nx)]
     out = call(columns_kernel, [], [*got, place], shape((slots, frames * part, features), bf16), [], 20, 400_000_000)

time: 96 us -> 98.9 us (1.030)
  Pallas kernels: 19.4 us -> 22 us
    pallas_call x8 -> x9, Pallas kernels: 19.4 us -> 22 us  [call(): pl.pallas_call(kernel, out_shape=outs, in_specs=[SMEM] * len(scalars) + [...]
  transfers between devices with their start and end apart: 20 -> 20, of which waited for: 5 -> 5; matrix products, arithmetic and copies ran while one was open for 0% -> 0% of each run, Pallas kernels for 15% -> 18%
where the time goes in v3:
time: 98.9 us; the launch traced here: 98.6 us
  starting transfers between devices  55 us (56%)
  Pallas kernels  22 us (22%)
  waiting for transfers between devices  15 us (15%)
  local copies, waits for them, and re-layouts  5.88 us (6%)
    pallas_call x9, Pallas kernels, call(): pl.pallas_call(kernel, out_shape=outs, in_specs=[SMEM] * len(scalars) + [...  22 us
    ppermute x4, starting transfers between devices, on_device(): feats[k] = from_one = lax.ppermute(to_one, 'rows', one)  16.3 us
    ppermute x7, starting transfers between devices, on_device(): lax.ppermute(pieces[d], 'rows', turned[d])  13.3 us
    all_to_all x1, starting transfers between devices, on_device(): lax.all_to_all(mine, 'roll', 0, 0, axis_index_groups=same_core, tiled=True)  13.2 us
    ppermute x3, starting transfers between devices, on_device(): came = lax.ppermute(lat, 'rows', [(i, i ^ bit) for i in range(nx)])  9.75 us
    ppermute x7, waiting for transfers between devices, on_device(): lax.ppermute(pieces[d], 'rows', turned[d])  5.56 us
    all_to_all x1, waiting for transfers between devices, on_device(): lax.all_to_all(mine, 'roll', 0, 0, axis_index_groups=same_core, tiled=True)  5.35 us
    unnamed x18, local copies, waits for them, and re-layouts  3.77 us
  transfers between devices with their start and end apart: 20, of which 5 were waited for; matrix products, arithmetic and copies ran while one was open for 0% of the time, Pallas kernels for 18%

profile of v3, /device:TPU:516, one launch (start us, length us, event | category | flops | bytes accessed | tf_op | source)
XLA Modules:
  0.0 98.6 jit_solution(499774791149542200)
XLA Ops:
  0.0 2.1 %broadcast_in_dim.16 = bf16[8,4,13824]{2,1,0:T(4,128)(2,1)} broadcast(bf16[4,13824]{1,0:T(4,128)(2,1)} %bitcast.12), dimensions={1,2} | broadcast | bytes 995328 | tf_op jit(solution)/shard_map/broadcast_in_dim | solution.py:338
  2.1 13.2 %all-to-all-start = ((bf16[8,4,13824]{2,1,0:T(4,128)(2,1)}), bf16[8,4,13824]{2,1,0:T(4,128)(2,1)S(1)}, u32[]{:S(2)}, u32[]{:S(2)}) async-start(bf16[8,4,13824]{2,1,0:T(4,128)(2,1)} %broadcast_in_dim.16), calls=%async_computation | async-start | bytes 1769472 | tf_op jit(solution)/shard_map/all_to_all | solution.py:339
  15.3 0.9 copy-done.1
  16.2 0.8 copy-done.2
  17.0 0.4 shard_map.100
  17.4 4.4 %collective-permute-start.8 = (bf16[1,2,5,8,128]{4,3,2,1,0:T(8,128)(2,1)S(1)}, bf16[1,2,5,8,128]{4,3,2,1,0:T(8,128)(2,1)S(1)}, u32[]{:S(2)}, u32[]{:S(2)}) collective-permute-start(bf16[1,2,5,8,128]{4,3,2,1,0:T(8,128)(2,1)S(1)} %shard_map.100), channel_id=1, source_target_pairs={{0,4},{1,5},{2,6},{3,7},{4,0},{5,1},{6,2},{7,3},{8,12},{9,13},{10,... | collective-permute-start | bytes 61448 | tf_op jit(solution)/shard_map/ppermute | solution.py:317
  21.8 1.3 %collective-permute-start = (bf16[2,2,64,512]{3,2,1,0:T(8,128)(2,1)}, bf16[2,2,64,512]{3,2,1,0:T(8,128)(2,1)S(1)}, u32[]{:S(2)}, u32[]{:S(2)}) collective-permute-start(bf16[2,2,64,512]{3,2,1,0:T(8,128)(2,1)} %bitcast.9), channel_id=1, source_target_pairs={{0,7},{1,2},{2,1},{3,4},{4,3},{5,6},{6,5},{7,0},{8,15},{9,10},{10,... | collective-permute-start | bytes 786440 | tf_op jit(solution)/shard_map/ppermute | solution.py:333
  23.1 8.4 %collective-permute-start.4 = (bf16[2,2,64,512]{3,2,1,0:T(8,128)(2,1)}, bf16[2,2,64,512]{3,2,1,0:T(8,128)(2,1)S(1)}, u32[]{:S(2)}, u32[]{:S(2)}) collective-permute-start(bf16[2,2,64,512]{3,2,1,0:T(8,128)(2,1)} %bitcast.10), channel_id=1, source_target_pairs={{0,1},{1,0},{2,3},{3,2},{4,5},{5,4},{6,7},{7,6},{8,9},{9,8},{10,11... | collective-permute-start | bytes 786440 | tf_op jit(solution)/shard_map/ppermute | solution.py:332
  31.5 0.0 collective-permute-done.8
  31.5 3.7 %collective-permute-start.9 = (bf16[2,2,5,8,128]{4,3,2,1,0:T(8,128)(2,1)S(1)}, bf16[2,2,5,8,128]{4,3,2,1,0:T(8,128)(2,1)S(1)}, u32[]{:S(2)}, u32[]{:S(2)}) collective-permute-start(bf16[2,2,5,8,128]{4,3,2,1,0:T(8,128)(2,1)S(1)} %pad_maximum_fusion.1), channel_id=1, source_target_pairs={{0,2},{1,3},{2,0},{3,1},{4,6},{5,7},{6,4},{7,5},{8,10},{9,11},{10,... | collective-permute-start | bytes 122888 | tf_op jit(solution)/shard_map/ppermute | solution.py:317
  35.2 5.4 %all-to-all-done.mine_ref = bf16[8,4,13824]{2,1,0:T(4,128)(2,1)S(1)} async-done(((bf16[8,4,13824]{2,1,0:T(4,128)(2,1)}), bf16[8,4,13824]{2,1,0:T(4,128)(2,1)S(1)}, u32[]{:S(2)}, u32[]{:S(2)}) %all-to-all-start) | async-done | bytes 884768 | tf_op jit(solution)/shard_map/all_to_all | solution.py:339
  40.5 0.0 collective-permute-start.11
  40.6 0.0 collective-permute-done.9
  40.6 1.7 %collective-permute-start.10 = (bf16[4,2,5,8,128]{4,3,2,1,0:T(8,128)(2,1)S(1)}, bf16[4,2,5,8,128]{4,3,2,1,0:T(8,128)(2,1)S(1)}, u32[]{:S(2)}, u32[]{:S(2)}) collective-permute-start(bf16[4,2,5,8,128]{4,3,2,1,0:T(8,128)(2,1)S(1)} %pad_maximum_fusion.refs_1_), channel_id=1, source_target_pairs={{0,1},{1,0},{2,3},{3,2},{4,5},{5,4},{6,7},{7,6},{8,9},{9,8},{10,11... | collective-permute-start | bytes 245768 | tf_op jit(solution)/shard_map/ppermute | solution.py:317
  42.3 0.7 copy-done.3
  43.0 0.7 copy-done.4
  43.7 0.7 copy-done.5
  44.4 0.9 shard_map.101
  45.3 0.5 collective-permute-start.1
  45.8 0.0 collective-permute-done.4.refs_3_
  45.8 0.4 collective-permute-start.5
  46.2 0.0 collective-permute-done.10.refs_2_
  46.2 6.1 %shard_map.102 = (f32[2,3,512,512]{3,2,1,0:T(8,128)S(1)}, f32[3,512,128]{2,1,0:T(8,128)S(1)}, f32[16,512]{1,0:T(8,128)S(1)}) custom-call(s32[1]{0:T(128)} %bitcast.refs_0_, bf16[4,2,5,8,128]{4,3,2,1,0:T(8,128)(2,1)S(1)} %pad_maximum_fusion.refs_1_, bf16[4,2,5,8,128]{4,3,2,1,0:T(8,128)(2,1)S(1)} %collective-permute-done.10.refs_2_, ...), custom_call_target="tpu_custom_call" | custom-call | flops 5000000000 | bytes 4194304 | tf_op jit(solution)/shard_map/pallas_call | solution.py:262
  52.3 1.5 %collective-permute-done.1.refs_4_ = bf16[2,2,64,512]{3,2,1,0:T(8,128)(2,1)S(1)} collective-permute-done((bf16[2,2,64,512]{3,2,1,0:T(8,128)(2,1)S(1)}, bf16[2,2,64,512]{3,2,1,0:T(8,128)(2,1)S(1)}, u32[]{:S(2)}, u32[]{:S(2)}) %collective-permute-start.1) | collective-permute-done | bytes 262176 | tf_op jit(solution)/shard_map/ppermute | solution.py:332
  53.8 0.5 collective-permute-start.2
  54.3 0.0 collective-permute-done.5.refs_7_
  54.3 3.1 %collective-permute-start.6 = (bf16[2,2,64,512]{3,2,1,0:T(8,128)(2,1)S(1)}, bf16[2,2,64,512]{3,2,1,0:T(8,128)(2,1)S(1)}, u32[]{:S(2)}, u32[]{:S(2)}) collective-permute-start(bf16[2,2,64,512]{3,2,1,0:T(8,128)(2,1)S(1)} %collective-permute-done.5.refs_7_), channel_id=1, source_target_pairs={{0,1},{1,0},{2,3},{3,2},{4,5},{5,4},{6,7},{7,6},{8,9},{9,8},{10,11... | collective-permute-start | bytes 786440 | tf_op jit(solution)/shard_map/ppermute | solution.py:332
  57.4 1.4 %shard_map.103.act_ref = bf16[2,3,512,512]{3,2,1,0:T(8,128)(2,1)S(1)} custom-call(f32[2,3,512,512]{3,2,1,0:T(8,128)S(1)} %get-tuple-element.26.hid_ref, f32[16,512]{1,0:T(8,128)S(1)} %get-tuple-element.27.norm_ref), custom_call_target="tpu_custom_call" | custom-call | flops 3000000000 | bytes 4194304 | tf_op jit(solution)/shard_map/pallas_call | solution.py:262
  58.8 2.6 %collective-permute-done.2.refs_6_ = bf16[2,2,64,512]{3,2,1,0:T(8,128)(2,1)S(1)} collective-permute-done((bf16[2,2,64,512]{3,2,1,0:T(8,128)(2,1)S(1)}, bf16[2,2,64,512]{3,2,1,0:T(8,128)(2,1)S(1)}, u32[]{:S(2)}, u32[]{:S(2)}) %collective-permute-start.2) | collective-permute-done | bytes 262176 | tf_op jit(solution)/shard_map/ppermute | solution.py:333
  61.4 4.3 %collective-permute-start.3 = (bf16[1,2,64,512]{3,2,1,0:T(8,128)(2,1)S(1)}, bf16[1,2,64,512]{3,2,1,0:T(8,128)(2,1)S(1)}, u32[]{:S(2)}, u32[]{:S(2)}) collective-permute-start(bf16[1,2,64,512]{3,2,1,0:T(8,128)(2,1)S(1)} %slice.8), channel_id=1, source_target_pairs={{0,1},{1,0},{2,3},{3,2},{4,5},{5,4},{6,7},{7,6},{8,9},{9,8},{10,11... | collective-permute-start | bytes 393224 | tf_op jit(solution)/shard_map/ppermute | solution.py:332
  65.7 0.3 collective-permute-start.7
  66.0 2.8 %shard_map.104 = (f32[2,3,528,192]{3,2,1,0:T(8,128)S(1)}, bf16[64,13824]{1,0:T(8,128)(2,1)S(1)}) custom-call(bf16[2,3,512,512]{3,2,1,0:T(8,128)(2,1)S(1)} %shard_map.103.act_ref, bf16[8,4,13824]{2,1,0:T(4,128)(2,1)S(1)} %all-to-all-done.mine_ref, bf16[8,4,13824]{2,1,0:T(4,128)(2,1)S(1)} %collective-permute-done.11.other_ref), custom_call_target="tpu_custom_call" | custom-call | flops 3000000000 | bytes 4194304 | tf_op jit(solution)/shard_map/pallas_call | solution.py:262
  68.8 0.0 copy-start.8
  68.8 2.6 %shard_map.105.refs_10_ = f32[2,3,528,192]{3,2,1,0:T(8,128)S(1)} custom-call(bf16[2,3,512,512]{3,2,1,0:T(8,128)(2,1)S(1)} %shard_map.103.act_ref, bf16[64,13824]{1,0:T(8,128)(2,1)S(1)} %get-tuple-element.28.w_ref.refs_9_.refs_6_, f32[2,3,528,192]{3,2,1,0:T(8,128)S(1)} %get-tuple-element.30._), custom_call_target="tpu_custom_call", output_to_operand_aliasing={{}: (2, {})} | custom-call | flops 3000000000 | bytes 4194304 | tf_op jit(solution)/shard_map/pallas_call | solution.py:262
  71.4 0.0 copy-start.6
  71.5 0.0 copy-start.7
  71.5 3.4 %shard_map.106.refs_8_ = f32[2,3,528,192]{3,2,1,0:T(8,128)S(1)} custom-call(s32[1]{0:T(128)} %bitcast.refs_0_, s32[2]{0:T(128)S(1)} %copy-done.5, bf16[2,2,64,512]{3,2,1,0:T(8,128)(2,1)S(1)} %bitcast.11, bf16[2,2,64,512]{3,2,1,0:T(8,128)(2,1)S(1)} %collective-permute-done.4.refs_3_, ...), custom_call_target="tpu_custom_call", output_to_operand_aliasing={{}: (10, {})} | custom-call | flops 3000000000 | bytes 4194304 | tf_op jit(solution)/shard_map/pallas_call | solution.py:262
  74.9 3.1 %shard_map.107 = (bf16[3,64,128]{2,1,0:T(8,128)(2,1)S(1)}, bf16[3,64,128]{2,1,0:T(8,128)(2,1)S(1)}, bf16[3,64,128]{2,1,0:T(8,128)(2,1)S(1)}, bf16[3,64,128]{2,1,...) custom-call(s32[1]{0:T(128)} %bitcast.refs_0_, ...), custom_call_target="tpu_custom_call", output_to_operand_aliasing={{8}: (8, {})} | custom-call | flops 1000000000 | bytes 4194304 | tf_op jit(solution)/shard_map/pallas_call | solution.py:262
  77.9 1.6 %collective-permute-start.12 = (bf16[3,64,128]{2,1,0:T(8,128)(2,1)S(1)}, bf16[3,64,128]{2,1,0:T(8,128)(2,1)S(1)}, u32[]{:S(2)}, u32[]{:S(2)}) collective-permute-start(bf16[3,64,128]{2,1,0:T(8,128)(2,1)S(1)} %get-tuple-element.32), channel_id=1, source_target_pairs={{0,1},{1,2},{2,3},{3,4},{4,5},{5,6},{6,7},{7,0},{8,9},{9,10},{10,1... | collective-permute-start | bytes 147464 | tf_op jit(solution)/shard_map/ppermute | solution.py:407
  79.5 1.2 %collective-permute-start.13 = (bf16[3,64,128]{2,1,0:T(8,128)(2,1)S(1)}, bf16[3,64,128]{2,1,0:T(8,128)(2,1)S(1)}, u32[]{:S(2)}, u32[]{:S(2)}) collective-permute-start(bf16[3,64,128]{2,1,0:T(8,128)(2,1)S(1)} %get-tuple-element.33), channel_id=1, source_target_pairs={{0,2},{1,3},{2,4},{3,5},{4,6},{5,7},{6,0},{7,1},{8,10},{9,11},{10,... | collective-permute-start | bytes 147464 | tf_op jit(solution)/shard_map/ppermute | solution.py:407
  80.8 2.8 %collective-permute-start.14 = (bf16[3,64,128]{2,1,0:T(8,128)(2,1)S(1)}, bf16[3,64,128]{2,1,0:T(8,128)(2,1)S(1)}, u32[]{:S(2)}, u32[]{:S(2)}) collective-permute-start(bf16[3,64,128]{2,1,0:T(8,128)(2,1)S(1)} %get-tuple-element.34), channel_id=1, source_target_pairs={{0,3},{1,4},{2,5},{3,6},{4,7},{5,0},{6,1},{7,2},{8,11},{9,12},{10,... | collective-permute-start | bytes 147464 | tf_op jit(solution)/shard_map/ppermute | solution.py:407
  83.6 3.9 %collective-permute-start.15 = (bf16[3,64,128]{2,1,0:T(8,128)(2,1)S(1)}, bf16[3,64,128]{2,1,0:T(8,128)(2,1)S(1)}, u32[]{:S(2)}, u32[]{:S(2)}) collective-permute-start(bf16[3,64,128]{2,1,0:T(8,128)(2,1)S(1)} %get-tuple-element.35), channel_id=1, source_target_pairs={{0,4},{1,5},{2,6},{3,7},{4,0},{5,1},{6,2},{7,3},{8,12},{9,13},{10,... | collective-permute-start | bytes 147464 | tf_op jit(solution)/shard_map/ppermute | solution.py:407
  87.5 2.9 %collective-permute-start.16 = (bf16[3,64,128]{2,1,0:T(8,128)(2,1)S(1)}, bf16[3,64,128]{2,1,0:T(8,128)(2,1)S(1)}, u32[]{:S(2)}, u32[]{:S(2)}) collective-permute-start(bf16[3,64,128]{2,1,0:T(8,128)(2,1)S(1)} %get-tuple-element.36), channel_id=1, source_target_pairs={{0,5},{1,6},{2,7},{3,0},{4,1},{5,2},{6,3},{7,4},{8,13},{9,14},{10,... | collective-permute-start | bytes 147464 | tf_op jit(solution)/shard_map/ppermute | solution.py:407
  90.4 0.9 collective-permute-start.18
  91.2 0.4 fusion.refs_8_
  91.7 3.5 %collective-permute-done.16.refs_5_ = bf16[3,64,128]{2,1,0:T(8,128)(2,1)S(1)} collective-permute-done((bf16[3,64,128]{2,1,0:T(8,128)(2,1)S(1)}, bf16[3,64,128]{2,1,0:T(8,128)(2,1)S(1)}, u32[]{:S(2)}, u32[]{:S(2)}) %collective-permute-start.16) | collective-permute-done | bytes 49184 | tf_op jit(solution)/shard_map/ppermute | solution.py:407
  95.1 2.1 %collective-permute-done.17.refs_6_ = bf16[3,64,128]{2,1,0:T(8,128)(2,1)S(1)} collective-permute-done((bf16[3,64,128]{2,1,0:T(8,128)(2,1)S(1)}, bf16[3,64,128]{2,1,0:T(8,128)(2,1)S(1)}, u32[]{:S(2)}, u32[]{:S(2)}) %collective-permute-start.17) | collective-permute-done | bytes 49184 | tf_op jit(solution)/shard_map/ppermute | solution.py:407
  97.2 1.3 %shard_map.108 = bf16[2,192,512]{2,1,0:T(8,128)(2,1)} custom-call(bf16[3,64,128]{2,1,0:T(8,128)(2,1)S(1)} %get-tuple-element.31.refs_0_, bf16[3,64,128]{2,1,0:T(8,128)(2,1)S(1)} %collective-permute-done.12.refs_1_, bf16[3,64,128]{2,1,0:T(8,128)(2,1)S(1)} %collective-permute-done.13.refs_2_, bf16[3,64,128]{2,1,0:T(8,128)(2,1)S(1)} %collective-permute-done.14.refs_3_, ...), custom_call_target="tpu_custom_call" | custom-call | flops 400000000 | bytes 4194304 | tf_op jit(solution)/shard_map/pallas_call | solution.py:262
  (26 shorter events, 0.1 us)
Async XLA Ops:
  0.0 42.3 %copy-start = (bf16[432,512]{1,0:T(8,128)(2,1)S(1)}, bf16[432,512]{1,0:T(8,128)(2,1)}, u32[]{:S(2)}) copy-start(bf16[432,512]{1,0:T(8,128)(2,1)} %refs_3_.2) | copy-start | bytes 1327108
  2.1 38.4 %all-to-all-start = ((bf16[8,4,13824]{2,1,0:T(4,128)(2,1)}), bf16[8,4,13824]{2,1,0:T(4,128)(2,1)S(1)}, u32[]{:S(2)}, u32[]{:S(2)}) async-start(bf16[8,4,13824]{2,1,0:T(4,128)(2,1)} %broadcast_in_dim.16), calls=%async_computation | async-start | bytes 1769472 | tf_op jit(solution)/shard_map/all_to_all | solution.py:339
  15.3 0.9 copy-start.1
  16.2 0.8 copy-start.2
  17.4 14.1 %collective-permute-start.8 = (bf16[1,2,5,8,128]{4,3,2,1,0:T(8,128)(2,1)S(1)}, bf16[1,2,5,8,128]{4,3,2,1,0:T(8,128)(2,1)S(1)}, u32[]{:S(2)}, u32[]{:S(2)}) collective-permute-start(bf16[1,2,5,8,128]{4,3,2,1,0:T(8,128)(2,1)S(1)} %shard_map.100), channel_id=1, source_target_pairs={{0,4},{1,5},{2,6},{3,7},{4,0},{5,1},{6,2},{7,3},{8,12},{9,13},{10,... | collective-permute-start | bytes 61448 | tf_op jit(solution)/shard_map/ppermute | solution.py:317
  21.8 23.5 %collective-permute-start = (bf16[2,2,64,512]{3,2,1,0:T(8,128)(2,1)}, bf16[2,2,64,512]{3,2,1,0:T(8,128)(2,1)S(1)}, u32[]{:S(2)}, u32[]{:S(2)}) collective-permute-start(bf16[2,2,64,512]{3,2,1,0:T(8,128)(2,1)} %bitcast.9), channel_id=1, source_target_pairs={{0,7},{1,2},{2,1},{3,4},{4,3},{5,6},{6,5},{7,0},{8,15},{9,10},{10,... | collective-permute-start | bytes 786440 | tf_op jit(solution)/shard_map/ppermute | solution.py:333
  23.1 22.7 %collective-permute-start.4 = (bf16[2,2,64,512]{3,2,1,0:T(8,128)(2,1)}, bf16[2,2,64,512]{3,2,1,0:T(8,128)(2,1)S(1)}, u32[]{:S(2)}, u32[]{:S(2)}) collective-permute-start(bf16[2,2,64,512]{3,2,1,0:T(8,128)(2,1)} %bitcast.10), channel_id=1, source_target_pairs={{0,1},{1,0},{2,3},{3,2},{4,5},{5,4},{6,7},{7,6},{8,9},{9,8},{10,11... | collective-permute-start | bytes 786440 | tf_op jit(solution)/shard_map/ppermute | solution.py:332
  31.5 9.0 %collective-permute-start.9 = (bf16[2,2,5,8,128]{4,3,2,1,0:T(8,128)(2,1)S(1)}, bf16[2,2,5,8,128]{4,3,2,1,0:T(8,128)(2,1)S(1)}, u32[]{:S(2)}, u32[]{:S(2)}) collective-permute-start(bf16[2,2,5,8,128]{4,3,2,1,0:T(8,128)(2,1)S(1)} %pad_maximum_fusion.1), channel_id=1, source_target_pairs={{0,2},{1,3},{2,0},{3,1},{4,6},{5,7},{6,4},{7,5},{8,10},{9,11},{10,... | collective-permute-start | bytes 122888 | tf_op jit(solution)/shard_map/ppermute | solution.py:317
  40.5 25.4 %collective-permute-start.11 = (bf16[8,4,13824]{2,1,0:T(4,128)(2,1)S(1)}, bf16[8,4,13824]{2,1,0:T(4,128)(2,1)S(1)}, u32[]{:S(2)}, u32[]{:S(2)}) collective-permute-start(bf16[8,4,13824]{2,1,0:T(4,128)(2,1)S(1)} %all-to-all-done.mine_ref), channel_id=1, source_target_pairs={{0,8},{8,0},{16,24},{24,16},{32,40},{40,32},{48,56},{56,48},{64,72... | collective-permute-start | bytes 2654216 | tf_op jit(solution)/shard_map/ppermute | solution.py:340
  40.6 5.6 %collective-permute-start.10 = (bf16[4,2,5,8,128]{4,3,2,1,0:T(8,128)(2,1)S(1)}, bf16[4,2,5,8,128]{4,3,2,1,0:T(8,128)(2,1)S(1)}, u32[]{:S(2)}, u32[]{:S(2)}) collective-permute-start(bf16[4,2,5,8,128]{4,3,2,1,0:T(8,128)(2,1)S(1)} %pad_maximum_fusion.refs_1_), channel_id=1, source_target_pairs={{0,1},{1,0},{2,3},{3,2},{4,5},{5,4},{6,7},{7,6},{8,9},{9,8},{10,11... | collective-permute-start | bytes 245768 | tf_op jit(solution)/shard_map/ppermute | solution.py:317
  42.3 0.7 copy-start.3
  43.0 0.7 copy-start.4
  43.7 0.7 copy-start.5
  45.3 8.5 %collective-permute-start.1 = (bf16[2,2,64,512]{3,2,1,0:T(8,128)(2,1)S(1)}, bf16[2,2,64,512]{3,2,1,0:T(8,128)(2,1)S(1)}, u32[]{:S(2)}, u32[]{:S(2)}) collective-permute-start(bf16[2,2,64,512]{3,2,1,0:T(8,128)(2,1)S(1)} %collective-permute-done.refs_8_), channel_id=1, source_target_pairs={{0,1},{1,0},{2,3},{3,2},{4,5},{5,4},{6,7},{7,6},{8,9},{9,8},{10,11... | collective-permute-start | bytes 786440 | tf_op jit(solution)/shard_map/ppermute | solution.py:332
  45.8 8.5 %collective-permute-start.5 = (bf16[2,2,64,512]{3,2,1,0:T(8,128)(2,1)S(1)}, bf16[2,2,64,512]{3,2,1,0:T(8,128)(2,1)S(1)}, u32[]{:S(2)}, u32[]{:S(2)}) collective-permute-start(bf16[2,2,64,512]{3,2,1,0:T(8,128)(2,1)S(1)} %collective-permute-done.4.refs_3_), channel_id=1, source_target_pairs={{0,7},{1,2},{2,1},{3,4},{4,3},{5,6},{6,5},{7,0},{8,15},{9,10},{10,... | collective-permute-start | bytes 786440 | tf_op jit(solution)/shard_map/ppermute | solution.py:333
  53.8 7.6 %collective-permute-start.2 = (bf16[2,2,64,512]{3,2,1,0:T(8,128)(2,1)S(1)}, bf16[2,2,64,512]{3,2,1,0:T(8,128)(2,1)S(1)}, u32[]{:S(2)}, u32[]{:S(2)}) collective-permute-start(bf16[2,2,64,512]{3,2,1,0:T(8,128)(2,1)S(1)} %collective-permute-done.1.refs_4_), channel_id=1, source_target_pairs={{0,7},{1,2},{2,1},{3,4},{4,3},{5,6},{6,5},{7,0},{8,15},{9,10},{10,... | collective-permute-start | bytes 786440 | tf_op jit(solution)/shard_map/ppermute | solution.py:333
  54.3 11.4 %collective-permute-start.6 = (bf16[2,2,64,512]{3,2,1,0:T(8,128)(2,1)S(1)}, bf16[2,2,64,512]{3,2,1,0:T(8,128)(2,1)S(1)}, u32[]{:S(2)}, u32[]{:S(2)}) collective-permute-start(bf16[2,2,64,512]{3,2,1,0:T(8,128)(2,1)S(1)} %collective-permute-done.5.refs_7_), channel_id=1, source_target_pairs={{0,1},{1,0},{2,3},{3,2},{4,5},{5,4},{6,7},{7,6},{8,9},{9,8},{10,11... | collective-permute-start | bytes 786440 | tf_op jit(solution)/shard_map/ppermute | solution.py:332
  61.4 13.5 %collective-permute-start.3 = (bf16[1,2,64,512]{3,2,1,0:T(8,128)(2,1)S(1)}, bf16[1,2,64,512]{3,2,1,0:T(8,128)(2,1)S(1)}, u32[]{:S(2)}, u32[]{:S(2)}) collective-permute-start(bf16[1,2,64,512]{3,2,1,0:T(8,128)(2,1)S(1)} %slice.8), channel_id=1, source_target_pairs={{0,1},{1,0},{2,3},{3,2},{4,5},{5,4},{6,7},{7,6},{8,9},{9,8},{10,11... | collective-permute-start | bytes 393224 | tf_op jit(solution)/shard_map/ppermute | solution.py:332
  65.7 9.2 %collective-permute-start.7 = (bf16[1,2,64,512]{3,2,1,0:T(8,128)(2,1)S(1)}, bf16[1,2,64,512]{3,2,1,0:T(8,128)(2,1)S(1)}, u32[]{:S(2)}, u32[]{:S(2)}) collective-permute-start(bf16[1,2,64,512]{3,2,1,0:T(8,128)(2,1)S(1)} %slice.9), channel_id=1, source_target_pairs={{0,7},{1,2},{2,1},{3,4},{4,3},{5,6},{6,5},{7,0},{8,15},{9,10},{10,... | collective-permute-start | bytes 393224 | tf_op jit(solution)/shard_map/ppermute | solution.py:333
  68.8 2.6 %copy-start.8 = (bf16[2,2,8,8,512]{4,3,2,1,0:T(8,128)(2,1)S(1)}, bf16[2,2,8,8,512]{4,3,2,1,0:T(8,128)(2,1)}, u32[]{:S(2)}) copy-start(bf16[2,2,8,8,512]{4,3,2,1,0:T(8,128)(2,1)} %param.12) | copy-start | bytes 786436
  71.4 3.4 %copy-start.6 = (s32[2]{0:T(128)S(1)}, s32[2]{0:T(128)}, u32[]{:S(2)}) copy-start(s32[2]{0:T(128)} %refs_2_.3) | copy-start | bytes 28
  71.5 3.4 %copy-start.7 = (s32[2]{0:T(128)S(1)}, s32[2]{0:T(128)}, u32[]{:S(2)}) copy-start(s32[2]{0:T(128)} %refs_3_.3) | copy-start | bytes 28
  77.9 12.4 %collective-permute-start.12 = (bf16[3,64,128]{2,1,0:T(8,128)(2,1)S(1)}, bf16[3,64,128]{2,1,0:T(8,128)(2,1)S(1)}, u32[]{:S(2)}, u32[]{:S(2)}) collective-permute-start(bf16[3,64,128]{2,1,0:T(8,128)(2,1)S(1)} %get-tuple-element.32), channel_id=1, source_target_pairs={{0,1},{1,2},{2,3},{3,4},{4,5},{5,6},{6,7},{7,0},{8,9},{9,10},{10,1... | collective-permute-start | bytes 147464 | tf_op jit(solution)/shard_map/ppermute | solution.py:407
  79.5 10.8 %collective-permute-start.13 = (bf16[3,64,128]{2,1,0:T(8,128)(2,1)S(1)}, bf16[3,64,128]{2,1,0:T(8,128)(2,1)S(1)}, u32[]{:S(2)}, u32[]{:S(2)}) collective-permute-start(bf16[3,64,128]{2,1,0:T(8,128)(2,1)S(1)} %get-tuple-element.33), channel_id=1, source_target_pairs={{0,2},{1,3},{2,4},{3,5},{4,6},{5,7},{6,0},{7,1},{8,10},{9,11},{10,... | collective-permute-start | bytes 147464 | tf_op jit(solution)/shard_map/ppermute | solution.py:407
  80.8 10.9 %collective-permute-start.14 = (bf16[3,64,128]{2,1,0:T(8,128)(2,1)S(1)}, bf16[3,64,128]{2,1,0:T(8,128)(2,1)S(1)}, u32[]{:S(2)}, u32[]{:S(2)}) collective-permute-start(bf16[3,64,128]{2,1,0:T(8,128)(2,1)S(1)} %get-tuple-element.34), channel_id=1, source_target_pairs={{0,3},{1,4},{2,5},{3,6},{4,7},{5,0},{6,1},{7,2},{8,11},{9,12},{10,... | collective-permute-start | bytes 147464 | tf_op jit(solution)/shard_map/ppermute | solution.py:407
  83.6 8.1 %collective-permute-start.15 = (bf16[3,64,128]{2,1,0:T(8,128)(2,1)S(1)}, bf16[3,64,128]{2,1,0:T(8,128)(2,1)S(1)}, u32[]{:S(2)}, u32[]{:S(2)}) collective-permute-start(bf16[3,64,128]{2,1,0:T(8,128)(2,1)S(1)} %get-tuple-element.35), channel_id=1, source_target_pairs={{0,4},{1,5},{2,6},{3,7},{4,0},{5,1},{6,2},{7,3},{8,12},{9,13},{10,... | collective-permute-start | bytes 147464 | tf_op jit(solution)/shard_map/ppermute | solution.py:407
  87.5 7.7 %collective-permute-start.16 = (bf16[3,64,128]{2,1,0:T(8,128)(2,1)S(1)}, bf16[3,64,128]{2,1,0:T(8,128)(2,1)S(1)}, u32[]{:S(2)}, u32[]{:S(2)}) collective-permute-start(bf16[3,64,128]{2,1,0:T(8,128)(2,1)S(1)} %get-tuple-element.36), channel_id=1, source_target_pairs={{0,5},{1,6},{2,7},{3,0},{4,1},{5,2},{6,3},{7,4},{8,13},{9,14},{10,... | collective-permute-start | bytes 147464 | tf_op jit(solution)/shard_map/ppermute | solution.py:407
  90.4 6.9 %collective-permute-start.17 = (bf16[3,64,128]{2,1,0:T(8,128)(2,1)S(1)}, bf16[3,64,128]{2,1,0:T(8,128)(2,1)S(1)}, u32[]{:S(2)}, u32[]{:S(2)}) collective-permute-start(bf16[3,64,128]{2,1,0:T(8,128)(2,1)S(1)} %get-tuple-element.37), channel_id=1, source_target_pairs={{0,6},{1,7},{2,0},{3,1},{4,2},{5,3},{6,4},{7,5},{8,14},{9,15},{10,... | collective-permute-start | bytes 147464 | tf_op jit(solution)/shard_map/ppermute | solution.py:407
  90.4 6.9 %collective-permute-start.18 = (bf16[3,64,128]{2,1,0:T(8,128)(2,1)S(1)}, bf16[3,64,128]{2,1,0:T(8,128)(2,1)S(1)}, u32[]{:S(2)}, u32[]{:S(2)}) collective-permute-start(bf16[3,64,128]{2,1,0:T(8,128)(2,1)S(1)} %get-tuple-element.38), channel_id=1, source_target_pairs={{0,7},{1,0},{2,1},{3,2},{4,3},{5,4},{6,5},{7,6},{8,15},{9,8},{10,9... | collective-permute-start | bytes 147464 | tf_op jit(solution)/shard_map/ppermute | solution.py:407
